TPU v7x, 512 devices: a whole 4x4x16 slice. The times are simulated.
512 devices in a mesh: spec: 64 (over x_hi, z, core), img: 8 (over x_lo, y).
Axes of the slice: x: 4 (x_hi: 2, x_lo: 2; x = x_hi * 2 + x_lo), y: 4, z: 16, core: 2. Of those that a mesh axis runs over, the one named last changes fastest.
Arguments:
- spec_emb: bfloat16 [8192, 1024], P('spec', 'img'), may hold values from -1024 to 1024
- img_emb: bfloat16 [2048, 1024], P('img', 'spec'), may hold values from -16 to 16
- grad_spec: bfloat16 [8192, 1024], P('spec', 'img'), may hold values from -6 to 6
- grad_img: bfloat16 [2048, 1024], P('img', 'spec'), may hold values from -6 to 6
Outputs:
- spec_emb_grad: bfloat16 [8192, 1024], P('spec', 'img')
- img_emb_grad: bfloat16 [2048, 1024], P('img', 'spec')
All inputs are finite; a program needn't handle non-finite values.
Results may differ from a plain program's by a relative error of at most 0.0109.
Values may be sent and summed in bfloat16 or wider, within the bound.
No kernel may reach another device: no remote copies, remote signals or barrier semaphores. Data moves between devices by JAX's collectives and lax.ppermute only.
A program may use at most 64 MiB of HBM per device.

v0:
```python
import jax
import jax.numpy as jnp
from jax import lax
from jax.sharding import Mesh
from jax.sharding import PartitionSpec as P

D = 1024
HEADS = 16
SPEC = ("spec_0", "spec_1", "spec_2")


def collected_together(value, axis):
    leaves = jax.tree.leaves(value)
    order = sorted(range(len(leaves)), key=lambda k: -leaves[k].size)
    width = (1, *leaves[order[0]].shape)[-1]
    lines = [
        jnp.pad(leaves[k].reshape(-1), (0, -leaves[k].size % width)).reshape(-1, width)
        for k in order
    ]
    both, at, found = (lax.all_gather(jnp.concatenate(lines), axis), 0, {})
    for k, line in zip(order, lines):
        piece = both[:, at : at + len(line)].reshape(len(both), -1)
        found[k] = piece[:, : leaves[k].size].reshape(-1, *leaves[k].shape)
        at += len(line)
    numbers = iter(range(len(leaves)))
    return jax.tree.map(lambda _: found[next(numbers)], value)


def combined_by_axis(value, axes, combine):
    for axis in axes:
        pieces = collected_together(value, axis)
        value = jax.tree.map(lambda part: part[0], pieces)
        for k in range(1, lax.axis_size(axis)):
            value = combine(value, jax.tree.map(lambda part: part[k], pieces))
    return value


def turned_gather(arrays, axis, dims):
    turned = [jnp.moveaxis(a, dim, 0) for a, dim in zip(arrays, dims)]
    both = jnp.concatenate([t.reshape(len(t), -1) for t in turned], axis=1)
    whole, at, done = (lax.all_gather(both, axis, axis=0, tiled=True), 0, [])
    for t, dim in zip(turned, dims):
        piece = whole[:, at : at + t[0].size].reshape(-1, *t.shape[1:])
        done.append(jnp.moveaxis(piece, 0, dim))
        at += t[0].size
    return tuple(done)


def in_blocks(value, dim, peers):
    before, after = (value.shape[:dim], value.shape[dim + 1 :])
    return jnp.moveaxis(value.reshape(*before, peers, -1, *after), dim, 0)


def summed_on_arrival(value, axis, dim):
    peers = lax.axis_size(axis)
    pieces = lax.all_to_all(in_blocks(value, dim, peers), axis, 0, 0, tiled=True)
    return jnp.sum(pieces, axis=0)


def pair_combine(left_part, right_part):
    highest = jnp.maximum(left_part[0], right_part[0])
    left_factor = jnp.exp(left_part[0] - highest)
    right_factor = jnp.exp(right_part[0] - highest)
    return (
        highest,
        left_part[1] * left_factor + right_part[1] * right_factor,
        left_part[2] * left_factor + right_part[2] * right_factor,
    )


def local_moments(scores, moment, dim):
    highest = jnp.max(scores, axis=dim, keepdims=True)
    scaled = jnp.exp(scores - highest)
    return (
        highest,
        jnp.sum(scaled, axis=dim, keepdims=True),
        jnp.sum(scaled * moment, axis=dim, keepdims=True),
    )


def column_totals(scores, moment):
    highest, total, weighted = combined_by_axis(
        local_moments(scores, moment, 1), SPEC, pair_combine
    )
    weights = jnp.exp(scores - highest) / total
    delta = weighted / total
    return (weights, delta)


def local_row_totals(scores, moment):
    scaled = jnp.exp(scores - jnp.max(scores, axis=2, keepdims=True))
    weights = scaled / jnp.sum(scaled, axis=2, keepdims=True)
    return (weights, jnp.sum(weights * moment, axis=2, keepdims=True))


def score_block(spec_rows, spec_grad, image_rows, image_grad, row_rule, column_rule):
    scale = (D // HEADS) ** (-0.5)
    scores = (
        jnp.einsum("shd,ihd->hsi", spec_rows, image_rows, preferred_element_type=jnp.float32)
        * scale
    )
    row_moment = jnp.einsum(
        "shd,ihd->hsi", spec_grad, image_rows, preferred_element_type=jnp.float32
    )
    column_moment = jnp.einsum(
        "shd,ihd->hsi", spec_rows, image_grad, preferred_element_type=jnp.float32
    )
    row_weight, row_delta = row_rule(scores, row_moment)
    column_weight, column_delta = column_rule(scores, column_moment)
    slope = (
        row_weight * (row_moment - row_delta) + column_weight * (column_moment - column_delta)
    ).astype(jnp.bfloat16)
    spec_part = scale * jnp.einsum(
        "hsi,ihd->shd", slope, image_rows, preferred_element_type=jnp.float32
    )
    spec_part = spec_part + jnp.einsum(
        "hsi,ihd->shd",
        column_weight.astype(jnp.bfloat16),
        image_grad,
        preferred_element_type=jnp.float32,
    )
    image_part = scale * jnp.einsum(
        "hsi,shd->ihd", slope, spec_rows, preferred_element_type=jnp.float32
    )
    image_part = image_part + jnp.einsum(
        "hsi,shd->ihd",
        row_weight.astype(jnp.bfloat16),
        spec_grad,
        preferred_element_type=jnp.float32,
    )
    return (spec_part, image_part)


def shards(spec_emb, img_emb, grad_spec, grad_img):
    head_size = D // HEADS
    spec_count = spec_emb.shape[0]
    image_all, image_grad_all = turned_gather((img_emb, grad_img), SPEC, (1, 1))
    image_local, image_grad_local = (
        lax.all_to_all(image_all, "img", split_axis=1, concat_axis=0, tiled=True),
        lax.all_to_all(image_grad_all, "img", split_axis=1, concat_axis=0, tiled=True),
    )
    local_width = spec_emb.shape[1]
    local_heads = local_width // head_size
    image_count = image_local.shape[0]
    spec_heads = spec_emb.reshape(spec_count, local_heads, head_size)
    spec_grad_heads = grad_spec.reshape(spec_count, local_heads, head_size)
    image_heads = image_local.reshape(image_count, local_heads, head_size)
    image_grad_heads = image_grad_local.reshape(image_count, local_heads, head_size)
    spec_parts = []
    image_parts = []
    for head_index in range(local_heads):
        window = slice(head_index, head_index + 1)
        spec_part, image_part = score_block(
            spec_heads[:, window],
            spec_grad_heads[:, window],
            image_heads[:, window],
            image_grad_heads[:, window],
            local_row_totals,
            column_totals,
        )
        spec_parts.append(spec_part)
        image_parts.append(image_part)
    spec_result = (
        jnp.concatenate(spec_parts, axis=1).reshape(spec_count, local_width).astype(jnp.bfloat16)
    )
    image_total = jnp.concatenate(image_parts, axis=1).reshape(image_count, local_width)
    image_back = lax.all_to_all(image_total, "img", split_axis=0, concat_axis=1, tiled=True)
    image_result = summed_on_arrival(image_back, SPEC, 1).astype(jnp.bfloat16)
    return (spec_result, image_result)


def solution(mesh):
    split = Mesh(
        mesh.devices.reshape(2, 16, 2, mesh.shape["img"]), ("spec_0", "spec_1", "spec_2", "img")
    )
    return jax.shard_map(
        shards,
        mesh=split,
        in_specs=(P(SPEC, "img"), P("img", SPEC), P(SPEC, "img"), P("img", SPEC)),
        out_specs=(P(SPEC, "img"), P("img", SPEC)),
        check_vma=False,
    )
```

profile of v0, /device:TPU:1, one launch (start us, length us, event | category | flops | bytes accessed | tf_op | source)
XLA Modules:
  0.0 368.7 jit_solution(16061481993177456034)
XLA Ops:
  7.2 0.0 all-gather.14.cloned.1.call-start
  7.2 1.3 pad_maximum_fusion.2
  8.5 0.0 all-gather.14.cloned.1.call-update
  8.6 150.1 %all-gather.14.cloned.1.call-done = bf16[1024,512]{1,0:T(8,128)(2,1)} async-done(((bf16[16,512]{1,0:T(8,128)(2,1)}), bf16[1024,512]{1,0:T(8,128)(2,1)}) %all-gather.14.cloned.1.call-update) | async-done | bytes 1048592 | tf_op jit(solution)/shard_map/all_gather | solution.py:41
  158.7 2.3 fusion.160
  161.0 0.0 copy-start.5
  161.0 4.2 %all-to-all-start = ((bf16[256,8,128]{0,2,1:T(8,128)(2,1)}), bf16[256,8,128]{0,2,1:T(8,128)(2,1)S(1)}, u32[]{:S(2)}, u32[]{:S(2)}) async-start(bf16[256,8,128]{0,2,1:T(8,128)(2,1)} %bitcast.3), calls=%async_computation | async-start | bytes 1048576 | tf_op jit(solution)/shard_map/all_to_all | solution.py:139
  165.1 0.0 copy-done.5
  165.1 0.0 copy-start.6
  165.2 0.1 copy.22
  165.3 0.6 copy-done.6
  165.9 0.1 copy.23
  166.0 7.4 %all-to-all-done = bf16[256,8,128]{0,2,1:T(8,128)(2,1)S(1)} async-done(((bf16[256,8,128]{0,2,1:T(8,128)(2,1)}), bf16[256,8,128]{0,2,1:T(8,128)(2,1)S(1)}, u32[]{:S(2)}, u32[]{:S(2)}) %all-to-all-start) | async-done | bytes 524320 | tf_op jit(solution)/shard_map/all_to_all | solution.py:139
  173.4 4.7 %all-to-all-start.1 = ((bf16[256,8,128]{0,2,1:T(8,128)(2,1)}), bf16[256,8,128]{0,2,1:T(8,128)(2,1)S(1)}, u32[]{:S(2)}, u32[]{:S(2)}) async-start(bf16[256,8,128]{0,2,1:T(8,128)(2,1)} %bitcast.15), calls=%async_computation.1 | async-start | bytes 1048576 | tf_op jit(solution)/shard_map/all_to_all | solution.py:140
  178.1 0.3 copy.21
  178.4 0.2 reshape.515
  178.7 0.6 fusion.157
  179.3 0.6 fusion.156
  179.9 6.3 %all-to-all-done.1 = bf16[256,8,128]{0,2,1:T(8,128)(2,1)S(1)} async-done(((bf16[256,8,128]{0,2,1:T(8,128)(2,1)}), bf16[256,8,128]{0,2,1:T(8,128)(2,1)S(1)}, u32[]{:S(2)}, u32[]{:S(2)}) %all-to-all-start.1) | async-done | bytes 524320 | tf_op jit(solution)/shard_map/all_to_all | solution.py:140
  186.2 1.1 copy.24
  187.3 1.3 reshape.521
  188.6 0.0 copy-start.2
  188.6 1.1 fusion.12
  189.6 0.0 copy-done.2
  189.7 4.9 %all-gather.6 = f32[2,3,2048]{2,1,0:T(4,128)S(1)} all-gather(f32[1,3,2048]{2,1,0:T(4,128)S(1)} %maximum_bitcast_fusion), channel_id=2, replica_groups=mesh['spec_0'=2,'spec_1'=16,'spec_2'=2,'img'=8] {'spec_0'}, dimensions={0}, use_global_device_ids=true | all-gather | bytes 73728 | tf_op jit(solution)/shard_map/all_gather | solution.py:20
  194.7 23.2 %all-gather.7 = f32[16,3,2048]{2,1,0:T(4,128)S(1)} all-gather(f32[1,3,2048]{2,1,0:T(4,128)S(1)} %maximum_bitcast_fusion.1), channel_id=3, replica_groups=mesh['spec_0'=2,'spec_1'=16,'spec_2'=2,'img'=8] {'spec_1'}, dimensions={0}, use_global_device_ids=true | all-gather | bytes 417792 | tf_op jit(solution)/shard_map/all_gather | solution.py:20
  217.9 0.4 fusion.150
  218.3 0.4 fusion.151
  218.7 12.2 %all-gather.8 = f32[2,3,2048]{2,1,0:T(4,128)S(1)} all-gather(f32[1,3,2048]{2,1,0:T(4,128)S(1)} %maximum_bitcast_fusion.2), channel_id=4, replica_groups=mesh['spec_0'=2,'spec_1'=16,'spec_2'=2,'img'=8] {'spec_2'}, dimensions={0}, use_global_device_ids=true | all-gather | bytes 73728 | tf_op jit(solution)/shard_map/all_gather | solution.py:20
  231.0 0.1 fusion.84
  231.0 0.5 fusion.9
  231.5 1.5 fusion.8
  233.0 0.3 convolution_multiply_fusion.3
  233.3 0.0 copy-start.3
  233.3 0.3 fusion
  233.6 0.7 copy-done.3
  234.3 1.1 fusion.15
  235.4 4.9 %all-gather.9 = f32[2,3,2048]{2,1,0:T(4,128)S(1)} all-gather(f32[1,3,2048]{2,1,0:T(4,128)S(1)} %maximum_bitcast_fusion.3), channel_id=5, replica_groups=mesh['spec_0'=2,'spec_1'=16,'spec_2'=2,'img'=8] {'spec_0'}, dimensions={0}, use_global_device_ids=true | all-gather | bytes 73728 | tf_op jit(solution)/shard_map/all_gather | solution.py:20
  240.5 22.1 %all-gather.10 = f32[16,3,2048]{2,1,0:T(4,128)S(1)} all-gather(f32[1,3,2048]{2,1,0:T(4,128)S(1)} %maximum_bitcast_fusion.4), channel_id=6, replica_groups=mesh['spec_0'=2,'spec_1'=16,'spec_2'=2,'img'=8] {'spec_1'}, dimensions={0}, use_global_device_ids=true | all-gather | bytes 417792 | tf_op jit(solution)/shard_map/all_gather | solution.py:20
  262.5 0.4 fusion.152
  262.9 0.4 fusion.153
  263.4 10.3 %all-gather.11 = f32[2,3,2048]{2,1,0:T(4,128)S(1)} all-gather(f32[1,3,2048]{2,1,0:T(4,128)S(1)} %maximum_bitcast_fusion.5), channel_id=7, replica_groups=mesh['spec_0'=2,'spec_1'=16,'spec_2'=2,'img'=8] {'spec_2'}, dimensions={0}, use_global_device_ids=true | all-gather | bytes 73728 | tf_op jit(solution)/shard_map/all_gather | solution.py:20
  273.7 0.1 fusion.21
  273.7 0.5 fusion.7
  274.2 1.5 fusion.6
  275.7 0.0 copy-start
  275.7 0.3 convolution_multiply_fusion.2
  276.0 0.5 copy-done
  276.5 0.3 fusion.1
  276.8 0.1 pad_maximum_fusion
  276.9 0.3 copy.33
  277.3 0.3 copy.29
  277.6 17.9 %all_to_all.53 = f32[8,256,128]{1,2,0:T(8,128)} all-to-all(f32[8,256,128]{1,2,0:T(8,128)S(1)} %copy.29), channel_id=1, replica_groups=mesh['spec_0'=2,'spec_1'=16,'spec_2'=2,'img'=8] {'img'}, dimensions={0} | all-to-all | bytes 2097152 | tf_op jit(solution)/shard_map/all_to_all | solution.py:167
  295.5 12.8 %all-to-all-start.3 = ((f32[64,256,16]{1,2,0:T(8,128)}), f32[64,256,16]{1,2,0:T(8,128)}, u32[]{:S(2)}, u32[]{:S(2)}) async-start(f32[64,256,16]{1,2,0:T(8,128)} %bitcast.185), calls=%async_computation.3 | async-start | bytes 2097152 | tf_op jit(solution)/shard_map/all_to_all | solution.py:56
  308.2 0.0 copy-start.1
  308.3 0.2 convolution_multiply_fusion.5
  308.5 0.8 copy-done.1
  309.3 0.2 convolution_multiply_fusion.4
  309.5 0.8 copy-done.4
  310.3 0.8 fusion.5
  311.1 0.8 fusion.4
  311.9 0.7 copy.30
  312.6 47.4 %all-to-all-done.3 = f32[64,256,16]{1,2,0:T(8,128)} async-done(((f32[64,256,16]{1,2,0:T(8,128)}), f32[64,256,16]{1,2,0:T(8,128)}, u32[]{:S(2)}, u32[]{:S(2)}) %all-to-all-start.3) | async-done | bytes 1048608 | tf_op jit(solution)/shard_map/all_to_all | solution.py:56
  359.9 1.9 reduce_sum.101
  (12 shorter events, 0.3 us)
Async XLA Ops:
  7.2 151.5 %all-gather.14.cloned.1.call-start = ((), (), s32[]{:S(2)}) async-start(), calls=%async_computation.4 | async-start | bytes 1064960 | tf_op jit(solution)/shard_map/all_gather | solution.py:41
  161.0 4.2 %copy-start.5 = (bf16[128,128]{1,0:T(8,128)(2,1)S(1)}, bf16[128,128]{1,0:T(8,128)(2,1)}, u32[]{:S(2)}) copy-start(bf16[128,128]{1,0:T(8,128)(2,1)} %param.4) | copy-start | bytes 98308
  161.0 12.5 %all-to-all-start = ((bf16[256,8,128]{0,2,1:T(8,128)(2,1)}), bf16[256,8,128]{0,2,1:T(8,128)(2,1)S(1)}, u32[]{:S(2)}, u32[]{:S(2)}) async-start(bf16[256,8,128]{0,2,1:T(8,128)(2,1)} %bitcast.3), calls=%async_computation | async-start | bytes 1048576 | tf_op jit(solution)/shard_map/all_to_all | solution.py:139
  165.1 0.8 copy-start.6
  173.4 12.7 %all-to-all-start.1 = ((bf16[256,8,128]{0,2,1:T(8,128)(2,1)}), bf16[256,8,128]{0,2,1:T(8,128)(2,1)S(1)}, u32[]{:S(2)}, u32[]{:S(2)}) async-start(bf16[256,8,128]{0,2,1:T(8,128)(2,1)} %bitcast.15), calls=%async_computation.1 | async-start | bytes 1048576 | tf_op jit(solution)/shard_map/all_to_all | solution.py:140
  188.6 1.1 copy-start.2
  233.3 1.0 copy-start.3
  275.7 0.8 copy-start
  295.5 64.5 %all-to-all-start.3 = ((f32[64,256,16]{1,2,0:T(8,128)}), f32[64,256,16]{1,2,0:T(8,128)}, u32[]{:S(2)}, u32[]{:S(2)}) async-start(f32[64,256,16]{1,2,0:T(8,128)} %bitcast.185), calls=%async_computation.3 | async-start | bytes 2097152 | tf_op jit(solution)/shard_map/all_to_all | solution.py:56
  308.2 1.0 copy-start.1
  309.3 1.0 copy-start.4
Sparse Core Ops, SparseCore 0:
  11.8 146.7 all-gather.13
where the time goes:
time: 372 us; the launch traced here: 369 us
  waiting for transfers between devices  211 us (57%)
  blocking collectives  95.5 us (26%)
  starting transfers between devices  21.7 us (6%)
  between operations  14.3 us (4%)
  local copies, waits for them, and re-layouts  10.3 us (3%)
  other arithmetic  8.31 us (2%)
  matrix products  7.42 us (2%)
    all_gather x1, waiting for transfers between devices, turned_gather(): whole, at, done = (lax.all_gather(both, axis, axis=0, tiled=True), 0, [])  150 us
    all_gather x6, blocking collectives, collected_together(): both, at, found = (lax.all_gather(jnp.concatenate(lines), axis), 0, {})  77.6 us
    all_to_all x1, waiting for transfers between devices, summed_on_arrival(): lax.all_to_all(in_blocks(value, dim, peers), axis, 0, 0, tiled=True)  47.4 us
    all_to_all x1, blocking collectives, shards(): lax.all_to_all(image_total, 'img', split_axis=0, concat_axis=1, tiled=True)  17.9 us
    all_to_all x1, starting transfers between devices, summed_on_arrival(): lax.all_to_all(in_blocks(value, dim, peers), axis, 0, 0, tiled=True)  12.8 us
  transfers between devices with their start and end apart: 4, of which 4 were waited for; matrix products, arithmetic and copies ran while one was open for 1% of the time, Pallas kernels for 0%

commit v1 on v0

v1 whole, which is shorter than its diff:
```python
import jax
import jax.numpy as jnp
from jax import lax
from jax.sharding import Mesh
from jax.sharding import PartitionSpec as P

D = 1024
HEADS = 16
SIZE = D // HEADS
SPEC = ("xh", "z3", "z2", "z1", "z0", "co")
IMG = ("xl", "y1", "y0")
EVERY = SPEC + IMG
GROUP = ("z0", "co", "xl", "y1", "y0")
ROWS = ("z0", "xl", "y1", "y0")
SCALE = SIZE**-0.5


def head_moves():
    pairs = []
    for source in range(512):
        xh, z3, z2, z1, z0, co, xl, y1, y0 = ((source >> k) & 1 for k in range(8, -1, -1))
        target = 0
        for bit in (xl, y1, y0, co, z0, z1, xh, 1 - z3, 1 - z2):
            target = 2 * target + bit
        pairs.append((source, target))
    return pairs


def dot(a, b, dims):
    return lax.dot_general(a, b, (dims, ((), ())), preferred_element_type=jnp.float32)


def moments(scores, moment, dim):
    highest = jnp.max(scores, axis=dim, keepdims=True)
    scaled = jnp.exp(scores - highest)
    return jnp.stack(
        (
            highest.reshape(-1),
            jnp.sum(scaled, axis=dim),
            jnp.sum(scaled * moment, axis=dim),
        )
    )


def totals(parts):
    highest = jnp.max(parts[:, 0], axis=0)
    factor = jnp.exp(parts[:, 0] - highest)
    total = jnp.sum(parts[:, 1] * factor, axis=0)
    return highest, total, jnp.sum(parts[:, 2] * factor, axis=0) / total


def shards(spec_emb, img_emb, grad_spec, grad_img):
    moves = head_moves()
    tokens = img_emb.shape[0]
    half = tokens // 2
    rows = spec_emb.shape[0]
    by_head = jnp.stack(
        [
            jnp.concatenate([a[:, h * SIZE : (h + 1) * SIZE] for a in (spec_emb, grad_spec)], axis=1)
            for h in range(2)
        ]
    )
    own = lax.all_to_all(by_head, "co", 0, 0, tiled=True).reshape(2 * rows, 2 * SIZE)
    own = lax.ppermute(own, EVERY, moves)
    features = 2 * img_emb.shape[1]
    image = jnp.concatenate([img_emb, grad_img], axis=1).T.reshape(features, 2, half)
    image = jnp.moveaxis(image, 1, 0)[None, :, None]
    image = jnp.broadcast_to(image, (2, 2, 8, features, half)).reshape(32, features, half)
    image = lax.all_to_all(image, GROUP, 0, 0, tiled=True)
    image = image.reshape(4, 8, 2, features // 2, half).transpose(2, 0, 3, 1, 4).reshape(2, SIZE, 8 * half)
    image_rows, image_grad = image[0], image[1]
    both = lax.all_gather(own, "co", tiled=True)
    spec_rows, spec_grad = both[:, :SIZE], both[:, SIZE:]

    across = ((1,), (0,))
    scores = dot(spec_rows, image_rows, across) * SCALE
    row_moment = dot(spec_grad, image_rows, across)
    column_moment = dot(spec_rows, image_grad, across)
    column_part = moments(scores, column_moment, 0)
    row_part = moments(scores, row_moment, 1)
    column_parts = lax.all_to_all(
        jnp.broadcast_to(column_part, (16, *column_part.shape)), ROWS, 0, 0, tiled=True
    )
    row_parts = lax.all_gather(row_part, "co")
    row_high, row_total, row_delta = (t[:, None] for t in totals(row_parts))
    column_high, column_total, column_delta = (t[None, :] for t in totals(column_parts))
    row_weight = jnp.exp(scores - row_high) / row_total
    column_weight = jnp.exp(scores - column_high) / column_total
    slope = (
        row_weight * (row_moment - row_delta) + column_weight * (column_moment - column_delta)
    ).astype(jnp.bfloat16)
    row_weight = row_weight.astype(jnp.bfloat16)
    column_weight = column_weight.astype(jnp.bfloat16)
    last = ((1,), (1,))
    spec_part = SCALE * dot(image_rows, slope, last) + dot(image_grad, column_weight, last)
    first = ((0,), (0,))
    image_part = SCALE * dot(spec_rows, slope, first) + dot(spec_grad, row_weight, first)

    spec_part = spec_part.astype(jnp.bfloat16).reshape(SIZE, 2, 2 * rows)
    spec_parts = lax.all_to_all(jnp.moveaxis(spec_part, 1, 0), "co", 0, 0, tiled=True)
    spec_sum = jnp.sum(spec_parts.astype(jnp.float32), axis=0).astype(jnp.bfloat16)
    spec_back = lax.ppermute(spec_sum, EVERY, [(b, a) for a, b in moves])

    image_part = image_part.astype(jnp.bfloat16).reshape(4, SIZE // 4, 8, half)
    image_part = jnp.moveaxis(image_part, 2, 1).reshape(32, SIZE // 4, half)
    image_parts = lax.all_to_all(image_part, GROUP, 0, 0, tiled=True)
    image_parts = image_parts.reshape(2, 2, 8, SIZE // 4, half).astype(jnp.float32)
    image_sum = jnp.sum(image_parts, axis=(0, 2)).astype(jnp.bfloat16)
    image_result = jnp.moveaxis(image_sum, 1, 2).reshape(tokens, SIZE // 4)

    spec_back = jnp.moveaxis(spec_back.reshape(SIZE, 2, rows), 1, 0)
    spec_heads = lax.all_to_all(spec_back, "co", 0, 0, tiled=True)
    spec_result = spec_heads.reshape(2 * SIZE, rows).T
    return (spec_result, image_result)


def solution(mesh):
    split = Mesh(mesh.devices.reshape((2,) * 9), EVERY)
    return jax.shard_map(
        shards,
        mesh=split,
        in_specs=(P(SPEC, IMG), P(IMG, SPEC), P(SPEC, IMG), P(IMG, SPEC)),
        out_specs=(P(SPEC, IMG), P(IMG, SPEC)),
        check_vma=False,
    )
```

time: 372 us -> 98.8 us (0.27)
  waiting for transfers between devices: 211 us -> 23.2 us
  blocking collectives: 95.5 us -> 13.4 us
  starting transfers between devices: 21.7 us -> 43.4 us
  between operations: 14.3 us -> 0.8 us
  local copies, waits for them, and re-layouts: 10.3 us -> 5.45 us
    all_gather x1 -> x0, waiting for transfers between devices: 150 us -> none  [turned_gather(): whole, at, done = (lax.all_gather(both, axis, axis=0, tiled=True), 0, [])]
    all_gather x6 -> x2, blocking collectives: 77.6 us -> 4.01 us  [the longest x1 2.12 us: shards(): row_parts = lax.all_gather(row_part, 'co')]
    all_to_all x3 -> x4, waiting for transfers between devices: 61.1 us -> 11 us  [the longest x1 6.54 us: shards(): image_parts = lax.all_to_all(image_part, GROUP, 0, 0, tiled=True)]
    ppermute x0 -> x2, starting transfers between devices: none -> 13.7 us  [the longest x1 8.22 us: shards(): spec_back = lax.ppermute(spec_sum, EVERY, [(b, a) for a, b in moves])]
    ppermute x0 -> x2, waiting for transfers between devices: none -> 12.2 us  [the longest x1 12.2 us: shards(): own = lax.ppermute(own, EVERY, moves)]
    all_to_all x1 -> x2, blocking collectives: 17.9 us -> 9.4 us  [the longest x1 5.14 us: shards(): lax.all_to_all(jnp.moveaxis(spec_part, 1, 0), 'co', 0, 0, tiled=True)]
    all_to_all x3 -> x4, starting transfers between devices: 21.6 us -> 29.8 us  [the longest x1 10.1 us: shards(): lax.all_to_all(by_head, 'co', 0, 0, tiled=True).reshape(2 * rows, 2 * SIZE)]
    unnamed x18 -> x4, local copies, waits for them, and re-layouts: 4.76 us -> 0.75 us
  transfers between devices with their start and end apart: 4 -> 6, of which waited for: 4 -> 4; matrix products, arithmetic and copies ran while one was open for 1% -> 5% of each run, Pallas kernels for 0% -> 0%
where the time goes in v1:
time: 98.8 us; the launch traced here: 98 us
  starting transfers between devices  43.4 us (44%)
  waiting for transfers between devices  23.2 us (23%)
  blocking collectives  13.4 us (14%)
  matrix products  6.73 us (7%)
  local copies, waits for them, and re-layouts  5.45 us (6%)
  other arithmetic  5.04 us (5%)
    ppermute x1, waiting for transfers between devices, shards(): own = lax.ppermute(own, EVERY, moves)  12.2 us
    all_to_all x1, starting transfers between devices, shards(): lax.all_to_all(by_head, 'co', 0, 0, tiled=True).reshape(2 * rows, 2 * SIZE)  10.1 us
    all_to_all x1, starting transfers between devices, shards(): image_parts = lax.all_to_all(image_part, GROUP, 0, 0, tiled=True)  8.57 us
    ppermute x1, starting transfers between devices, shards(): spec_back = lax.ppermute(spec_sum, EVERY, [(b, a) for a, b in moves])  8.22 us
    all_to_all x1, starting transfers between devices, shards(): lax.all_to_all(jnp.broadcast_to(column_part, (16, *column_part.shape)), R...  7.17 us
    dot_general x7, matrix products, dot(): lax.dot_general(a, b, (dims, ((), ())), preferred_element_type=jnp.float32)  6.73 us
    all_to_all x1, waiting for transfers between devices, shards(): image_parts = lax.all_to_all(image_part, GROUP, 0, 0, tiled=True)  6.54 us
    ppermute x1, starting transfers between devices, shards(): own = lax.ppermute(own, EVERY, moves)  5.45 us
  transfers between devices with their start and end apart: 6, of which 4 were waited for; matrix products, arithmetic and copies ran while one was open for 5% of the time, Pallas kernels for 0%

profile of v1, /device:TPU:1, one launch (start us, length us, event | category | flops | bytes accessed | tf_op | source)
XLA Modules:
  0.0 98.0 jit_solution(12998405698137575988)
XLA Ops:
  0.6 0.9 fusion.39
  1.5 0.9 fusion.40
  2.5 0.1 maximum_bitcast_fusion
  2.6 0.6 pad_maximum_fusion
  3.2 10.1 %all-to-all-start.1 = ((bf16[2,128,128]{2,1,0:T(8,128)(2,1)}), bf16[2,128,128]{2,1,0:T(8,128)(2,1)S(1)}, u32[]{:S(2)}, u32[]{:S(2)}) async-start(bf16[2,128,128]{2,1,0:T(8,128)(2,1)} %pad_maximum_fusion), calls=%async_computation.1 | async-start | bytes 131072 | tf_op jit(solution)/shard_map/all_to_all | solution.py:63
  13.3 0.7 maximum_bitcast_fusion.2
  14.0 0.3 all-to-all-done.1
  14.4 0.7 broadcast_in_dim.6
  15.1 3.9 %all-to-all-start = ((bf16[32,32,128]{2,1,0:T(8,128)(2,1)}), bf16[32,32,128]{2,1,0:T(8,128)(2,1)S(1)}, u32[]{:S(2)}, u32[]{:S(2)}) async-start(bf16[32,32,128]{2,1,0:T(8,128)(2,1)} %bitcast.2), calls=%async_computation | async-start | bytes 524288 | tf_op jit(solution)/shard_map/all_to_all | solution.py:69
  19.0 5.5 %collective-permute-start = (bf16[256,128]{1,0:T(8,128)(2,1)S(1)}, bf16[256,128]{1,0:T(8,128)(2,1)S(1)}, u32[]{:S(2)}, u32[]{:S(2)}) collective-permute-start(bf16[256,128]{1,0:T(8,128)(2,1)S(1)} %bitcast.118), channel_id=1, source_target_pairs={{0,3},{1,67},{2,131},{3,195},{4,259},{5,323},{6,387},{7,451},{8,35... | collective-permute-start | bytes 196616 | tf_op jit(solution)/shard_map/ppermute | solution.py:64
  24.5 12.2 %collective-permute-done = bf16[256,128]{1,0:T(8,128)(2,1)S(1)} collective-permute-done((bf16[256,128]{1,0:T(8,128)(2,1)S(1)}, bf16[256,128]{1,0:T(8,128)(2,1)S(1)}, u32[]{:S(2)}, u32[]{:S(2)}) %collective-permute-start) | collective-permute-done | bytes 65568 | tf_op jit(solution)/shard_map/ppermute | solution.py:64
  36.7 1.9 %all_gather.9 = bf16[512,128]{1,0:T(8,128)(2,1)S(1)} all-gather(bf16[256,128]{1,0:T(8,128)(2,1)S(1)} %collective-permute-done), channel_id=1, replica_groups=mesh['xh'=2,'z3'=2,'z2'=2,'z1'=2,'z0'=2,'co'=2,'xl'=2,'y1'=2,'y0'=2] {'co'}, dimensions={0}, use_global_device_ids=true | all-gather | bytes 196608 | tf_op jit(solution)/shard_map/all_gather | solution.py:72
  38.6 0.0 all-to-all-done
  38.7 0.4 fusion.10
  39.1 0.0 copy-start
  39.1 0.5 fusion.36
  39.6 2.3 %fusion = (f32[512]{0:T(512)S(1)}, f32[512]{0:T(512)S(1)}, f32[1024]{0:T(1024)S(1)}, f32[1024]{0:T(1024)S(1)}, f32[512,1024]{1,0:T(8,128)}) fusion(f32[512,1024]{1,0:T(8,128)S(1)} %get-tuple-element.40, f32[512]{0:T(512)S(1)} %get-tuple-element.20, f32[512,1024]{1,0:T(8,128)S(1)} %fusion.10, f32[1024]{0:T(1024)S(1)} %get-tuple-element.21, ...), kind=kOutput, calls=%fused_computation.7 | convolution fusion | flops 71300096 | bytes 6572032 | tf_op jit(solution)/shard_map/dot_general | solution.py:30
  41.9 0.0 copy-done
  41.9 0.8 broadcast_in_dim.8
  42.7 7.2 %all-to-all-start.2 = ((f32[16,3,1024]{2,1,0:T(4,128)}), f32[16,3,1024]{2,1,0:T(4,128)S(1)}, u32[]{:S(2)}, u32[]{:S(2)}) async-start(f32[16,3,1024]{2,1,0:T(4,128)} %broadcast_in_dim.8), calls=%async_computation.2 | async-start | bytes 524288 | tf_op jit(solution)/shard_map/all_to_all | solution.py:81
  49.9 2.1 %all-gather.1 = f32[2,3,512]{2,1,0:T(4,128)S(1)} all-gather(f32[1,3,512]{2,1,0:T(4,128)S(1)} %maximum_bitcast_fusion.3), channel_id=2, replica_groups=mesh['xh'=2,'z3'=2,'z2'=2,'z1'=2,'z0'=2,'co'=2,'xl'=2,'y1'=2,'y0'=2] {'co'}, dimensions={0}, use_global_device_ids=true | all-gather | bytes 18432 | tf_op jit(solution)/shard_map/all_gather | solution.py:84
  52.1 1.3 %fusion.6 = f32[64,1024]{1,0:T(8,128)} fusion(bf16[512,128]{1,0:T(8,128)(2,1)S(1)} %all_gather.9, f32[512,1024]{1,0:T(8,128)S(1)} %get-tuple-element.40, f32[512]{0:T(512)S(1)} %get-tuple-element.24, f32[512]{0:T(512)S(1)} %get-tuple-element.37), kind=kOutput, calls=%fused_computation.17 | convolution fusion | flops 68681728 | bytes 2494464 | tf_op jit(solution)/shard_map/dot_general | solution.py:30
  53.4 4.1 %all-to-all-done.2 = f32[16,3,1024]{2,1,0:T(4,128)S(1)} async-done(((f32[16,3,1024]{2,1,0:T(4,128)}), f32[16,3,1024]{2,1,0:T(4,128)S(1)}, u32[]{:S(2)}, u32[]{:S(2)}) %all-to-all-start.2) | async-done | bytes 196640 | tf_op jit(solution)/shard_map/all_to_all | solution.py:81
  57.5 0.2 fusion.37
  57.6 0.1 fusion.27
  57.7 3.3 %add_convert_fusion = bf16[512,1024]{1,0:T(8,128)(2,1)S(1)} fusion(f32[512,1024]{1,0:T(8,128)} %copy-done, f32[512,1024]{1,0:T(8,128)} %get-tuple-element.41, f32[1024]{0:T(1024)S(1)} %div.35, f32[512]{0:T(512)S(1)} %div.32, f32[1024]{0:T(1024)S(1)} %get-tuple-element.22, f32[512,1024]{1,0:T(8,128)S(1)} %get-tuple-element.40, f32[1024]{0:T(1024)S(1)} %get-tuple-element.27, ...), kind=kLoop, calls=%fused_computation | loop fusion | flops 5242880 | bytes 7358464 | tf_op jit(solution)/shard_map/convert_element_type | solution.py:91
  61.0 0.4 convolution_multiply_fusion.2
  61.4 0.5 fusion.5
  61.9 5.1 %all_to_all.30 = bf16[2,64,256]{2,1,0:T(8,128)(2,1)S(1)} all-to-all(bf16[2,64,256]{2,1,0:T(8,128)(2,1)S(1)} %bitcast.115), channel_id=1, replica_groups=mesh['xh'=2,'z3'=2,'z2'=2,'z1'=2,'z0'=2,'co'=2,'xl'=2,'y1'=2,'y0'=2] {'co'}, dimensions={0} | all-to-all | bytes 131072 | tf_op jit(solution)/shard_map/all_to_all | solution.py:100
  67.1 8.2 %collective-permute-start.1 = (bf16[64,256]{1,0:T(8,128)(2,1)S(1)}, bf16[64,256]{1,0:T(8,128)(2,1)S(1)}, u32[]{:S(2)}, u32[]{:S(2)}) collective-permute-start(bf16[64,256]{1,0:T(8,128)(2,1)S(1)} %reduce_sum.104), channel_id=1, source_target_pairs={{3,0},{67,1},{131,2},{195,3},{259,4},{323,5},{387,6},{451,7},{35,8... | collective-permute-start | bytes 98312 | tf_op jit(solution)/shard_map/ppermute | solution.py:102
  75.3 1.3 %fusion.4 = bf16[8,8,8,128]{3,1,2,0:T(8,128)(2,1)S(1)} fusion(f32[64,1024]{1,0:T(8,128)} %fusion.6, bf16[512,1024]{1,0:T(8,128)(2,1)S(1)} %add_convert_fusion, bf16[512,128]{1,0:T(8,128)(2,1)S(1)} %all_gather.9), kind=kOutput, calls=%fused_computation.15 | convolution fusion | flops 67305472 | bytes 1572864 | tf_op jit(solution)/shard_map/dot_general | solution.py:30
  76.6 0.7 copy.71
  77.3 0.0 collective-permute-done.1
  77.3 4.3 %all_to_all.31 = bf16[2,64,128]{2,1,0:T(8,128)(2,1)S(1)} all-to-all(bf16[2,64,128]{2,1,0:T(8,128)(2,1)S(1)} %copy.70), channel_id=1, replica_groups=mesh['xh'=2,'z3'=2,'z2'=2,'z1'=2,'z0'=2,'co'=2,'xl'=2,'y1'=2,'y0'=2] {'co'}, dimensions={0} | all-to-all | bytes 65536 | tf_op jit(solution)/shard_map/all_to_all | solution.py:112
  81.6 8.6 %all-to-all-start.5 = ((bf16[32,16,128]{2,1,0:T(8,128)(2,1)}), bf16[32,16,128]{2,1,0:T(8,128)(2,1)S(1)}, u32[]{:S(2)}, u32[]{:S(2)}) async-start(bf16[32,16,128]{2,1,0:T(8,128)(2,1)} %bitcast.25), calls=%async_computation.5 | async-start | bytes 262144 | tf_op jit(solution)/shard_map/all_to_all | solution.py:106
  90.2 0.7 copy.73
  90.9 6.5 %all-to-all-done.5 = bf16[32,16,128]{2,1,0:T(8,128)(2,1)S(1)} async-done(((bf16[32,16,128]{2,1,0:T(8,128)(2,1)}), bf16[32,16,128]{2,1,0:T(8,128)(2,1)S(1)}, u32[]{:S(2)}, u32[]{:S(2)}) %all-to-all-start.5) | async-done | bytes 131104 | tf_op jit(solution)/shard_map/all_to_all | solution.py:106
  97.4 0.6 copy_bitcast_fusion.2
  (17 shorter events, 0.3 us)
Async XLA Ops:
  3.2 11.2 %all-to-all-start.1 = ((bf16[2,128,128]{2,1,0:T(8,128)(2,1)}), bf16[2,128,128]{2,1,0:T(8,128)(2,1)S(1)}, u32[]{:S(2)}, u32[]{:S(2)}) async-start(bf16[2,128,128]{2,1,0:T(8,128)(2,1)} %pad_maximum_fusion), calls=%async_computation.1 | async-start | bytes 131072 | tf_op jit(solution)/shard_map/all_to_all | solution.py:63
  15.1 23.5 %all-to-all-start = ((bf16[32,32,128]{2,1,0:T(8,128)(2,1)}), bf16[32,32,128]{2,1,0:T(8,128)(2,1)S(1)}, u32[]{:S(2)}, u32[]{:S(2)}) async-start(bf16[32,32,128]{2,1,0:T(8,128)(2,1)} %bitcast.2), calls=%async_computation | async-start | bytes 524288 | tf_op jit(solution)/shard_map/all_to_all | solution.py:69
  19.0 17.6 %collective-permute-start = (bf16[256,128]{1,0:T(8,128)(2,1)S(1)}, bf16[256,128]{1,0:T(8,128)(2,1)S(1)}, u32[]{:S(2)}, u32[]{:S(2)}) collective-permute-start(bf16[256,128]{1,0:T(8,128)(2,1)S(1)} %bitcast.118), channel_id=1, source_target_pairs={{0,3},{1,67},{2,131},{3,195},{4,259},{5,323},{6,387},{7,451},{8,35... | collective-permute-start | bytes 196616 | tf_op jit(solution)/shard_map/ppermute | solution.py:64
  39.1 2.8 %copy-start = (f32[512,1024]{1,0:T(8,128)}, f32[512,1024]{1,0:T(8,128)S(1)}, u32[]{:S(2)}) copy-start(f32[512,1024]{1,0:T(8,128)S(1)} %fusion.10) | copy-start | bytes 6291460
  42.7 14.8 %all-to-all-start.2 = ((f32[16,3,1024]{2,1,0:T(4,128)}), f32[16,3,1024]{2,1,0:T(4,128)S(1)}, u32[]{:S(2)}, u32[]{:S(2)}) async-start(f32[16,3,1024]{2,1,0:T(4,128)} %broadcast_in_dim.8), calls=%async_computation.2 | async-start | bytes 524288 | tf_op jit(solution)/shard_map/all_to_all | solution.py:81
  67.1 10.2 %collective-permute-start.1 = (bf16[64,256]{1,0:T(8,128)(2,1)S(1)}, bf16[64,256]{1,0:T(8,128)(2,1)S(1)}, u32[]{:S(2)}, u32[]{:S(2)}) collective-permute-start(bf16[64,256]{1,0:T(8,128)(2,1)S(1)} %reduce_sum.104), channel_id=1, source_target_pairs={{3,0},{67,1},{131,2},{195,3},{259,4},{323,5},{387,6},{451,7},{35,8... | collective-permute-start | bytes 98312 | tf_op jit(solution)/shard_map/ppermute | solution.py:102
  81.6 15.8 %all-to-all-start.5 = ((bf16[32,16,128]{2,1,0:T(8,128)(2,1)}), bf16[32,16,128]{2,1,0:T(8,128)(2,1)S(1)}, u32[]{:S(2)}, u32[]{:S(2)}) async-start(bf16[32,16,128]{2,1,0:T(8,128)(2,1)} %bitcast.25), calls=%async_computation.5 | async-start | bytes 262144 | tf_op jit(solution)/shard_map/all_to_all | solution.py:106

commit v2 on v1

--- a/solution.py
+++ b/solution.py
@@ -3,6 +3,7 @@
 from jax import lax
 from jax.sharding import Mesh
 from jax.sharding import PartitionSpec as P
+
 
 D = 1024
 HEADS = 16
@@ -54,13 +55,12 @@
     tokens = img_emb.shape[0]
     half = tokens // 2
     rows = spec_emb.shape[0]
-    by_head = jnp.stack(
-        [
-            jnp.concatenate([a[:, h * SIZE : (h + 1) * SIZE] for a in (spec_emb, grad_spec)], axis=1)
-            for h in range(2)
-        ]
+    second = lax.axis_index("co") == 1
+    own = lax.all_gather(jnp.concatenate([spec_emb, grad_spec], axis=1), "co", tiled=True)
+    own = jnp.concatenate(
+        [jnp.where(second, a[:, SIZE:], a[:, :SIZE]) for a in (own[:, : 2 * SIZE], own[:, 2 * SIZE :])],
+        axis=1,
     )
-    own = lax.all_to_all(by_head, "co", 0, 0, tiled=True).reshape(2 * rows, 2 * SIZE)
     own = lax.ppermute(own, EVERY, moves)
     features = 2 * img_emb.shape[1]
     image = jnp.concatenate([img_emb, grad_img], axis=1).T.reshape(features, 2, half)
@@ -96,9 +96,9 @@
     first = ((0,), (0,))
     image_part = SCALE * dot(spec_rows, slope, first) + dot(spec_grad, row_weight, first)
 
-    spec_part = spec_part.astype(jnp.bfloat16).reshape(SIZE, 2, 2 * rows)
-    spec_parts = lax.all_to_all(jnp.moveaxis(spec_part, 1, 0), "co", 0, 0, tiled=True)
-    spec_sum = jnp.sum(spec_parts.astype(jnp.float32), axis=0).astype(jnp.bfloat16)
+    spec_parts = lax.all_gather(spec_part.astype(jnp.bfloat16), "co")
+    spec_parts = jnp.where(second, spec_parts[:, :, 2 * rows :], spec_parts[:, :, : 2 * rows])
+    spec_sum = (spec_parts[0].astype(jnp.float32) + spec_parts[1]).astype(jnp.bfloat16)
     spec_back = lax.ppermute(spec_sum, EVERY, [(b, a) for a, b in moves])
 
     image_part = image_part.astype(jnp.bfloat16).reshape(4, SIZE // 4, 8, half)
@@ -108,14 +108,14 @@
     image_sum = jnp.sum(image_parts, axis=(0, 2)).astype(jnp.bfloat16)
     image_result = jnp.moveaxis(image_sum, 1, 2).reshape(tokens, SIZE // 4)
 
-    spec_back = jnp.moveaxis(spec_back.reshape(SIZE, 2, rows), 1, 0)
-    spec_heads = lax.all_to_all(spec_back, "co", 0, 0, tiled=True)
-    spec_result = spec_heads.reshape(2 * SIZE, rows).T
+    spec_heads = lax.all_gather(spec_back, "co", tiled=True)
+    spec_result = jnp.where(second, spec_heads[:, rows:], spec_heads[:, :rows]).T
     return (spec_result, image_result)
 
 
 def solution(mesh):
     split = Mesh(mesh.devices.reshape((2,) * 9), EVERY)
+
     return jax.shard_map(
         shards,
         mesh=split,

time: 98.8 us -> 85.7 us (0.87)
  the two profiles are of different devices: /device:TPU:1 before, /device:TPU:19 now
where the time goes in v2:
time: 85.7 us; the launch traced here: 85.2 us
  starting transfers between devices  44.7 us (52%)
  blocking collectives  13.8 us (16%)
  waiting for transfers between devices  11.9 us (14%)
  other arithmetic  5.32 us (6%)
  matrix products  5.09 us (6%)
  local copies, waits for them, and re-layouts  3.59 us (4%)
    ppermute x1, starting transfers between devices, shards(): own = lax.ppermute(own, EVERY, moves)  13.2 us
    all_to_all x1, starting transfers between devices, shards(): image = lax.all_to_all(image, GROUP, 0, 0, tiled=True)  9.54 us
    ppermute x1, starting transfers between devices, shards(): spec_back = lax.ppermute(spec_sum, EVERY, [(b, a) for a, b in moves])  8.66 us
    all_to_all x1, starting transfers between devices, shards(): image_parts = lax.all_to_all(image_part, GROUP, 0, 0, tiled=True)  8.16 us
    ppermute x1, waiting for transfers between devices, shards(): spec_back = lax.ppermute(spec_sum, EVERY, [(b, a) for a, b in moves])  5.3 us
    all_to_all x1, starting transfers between devices, shards(): lax.all_to_all(jnp.broadcast_to(column_part, (16, *column_part.shape)), R...  5.16 us
    dot_general x7, matrix products, dot(): lax.dot_general(a, b, (dims, ((), ())), preferred_element_type=jnp.float32)  5.09 us
    ppermute x1, waiting for transfers between devices, shards(): own = lax.ppermute(own, EVERY, moves)  4.94 us
  transfers between devices with their start and end apart: 5, of which 3 were waited for; matrix products, arithmetic and copies ran while one was open for 3% of the time, Pallas kernels for 0%

profile of v2, /device:TPU:19, one launch (start us, length us, event | category | flops | bytes accessed | tf_op | source)
XLA Modules:
  0.0 85.2 jit_solution(16123905222824724543)
XLA Ops:
  0.6 0.7 maximum_bitcast_fusion
  1.4 0.7 broadcast_in_dim.6
  2.1 9.5 %all-to-all-start = ((bf16[32,32,128]{2,1,0:T(8,128)(2,1)}), bf16[32,32,128]{2,1,0:T(8,128)(2,1)S(1)}, u32[]{:S(2)}, u32[]{:S(2)}) async-start(bf16[32,32,128]{2,1,0:T(8,128)(2,1)} %bitcast.2), calls=%async_computation | async-start | bytes 524288 | tf_op jit(solution)/shard_map/all_to_all | solution.py:69
  11.7 0.8 pad_maximum_fusion
  12.4 1.9 %all_gather.21 = bf16[256,256]{1,0:T(8,128)(2,1)S(1)} all-gather(bf16[128,256]{1,0:T(8,128)(2,1)S(1)} %pad_maximum_fusion), channel_id=1, replica_groups=mesh['xh'=2,'z3'=2,'z2'=2,'z1'=2,'z0'=2,'co'=2,'xl'=2,'y1'=2,'y0'=2] {'co'}, dimensions={0}, use_global_device_ids=true | all-gather | bytes 196608 | tf_op jit(solution)/shard_map/all_gather | solution.py:59
  14.3 0.1 slice_select_fusion.2
  14.5 0.1 pad_maximum_fusion.1
  14.5 13.2 %collective-permute-start = (bf16[256,128]{1,0:T(8,128)(2,1)S(1)}, bf16[256,128]{1,0:T(8,128)(2,1)S(1)}, u32[]{:S(2)}, u32[]{:S(2)}) collective-permute-start(bf16[256,128]{1,0:T(8,128)(2,1)S(1)} %pad_maximum_fusion.1), channel_id=1, source_target_pairs={{0,3},{1,67},{2,131},{3,195},{4,259},{5,323},{6,387},{7,451},{8,35... | collective-permute-start | bytes 196616 | tf_op jit(solution)/shard_map/ppermute | solution.py:64
  27.7 4.9 %collective-permute-done = bf16[256,128]{1,0:T(8,128)(2,1)S(1)} collective-permute-done((bf16[256,128]{1,0:T(8,128)(2,1)S(1)}, bf16[256,128]{1,0:T(8,128)(2,1)S(1)}, u32[]{:S(2)}, u32[]{:S(2)}) %collective-permute-start) | collective-permute-done | bytes 65568 | tf_op jit(solution)/shard_map/ppermute | solution.py:64
  32.7 3.4 %all_gather.22 = bf16[512,128]{1,0:T(8,128)(2,1)S(1)} all-gather(bf16[256,128]{1,0:T(8,128)(2,1)S(1)} %collective-permute-done), channel_id=1, replica_groups=mesh['xh'=2,'z3'=2,'z2'=2,'z1'=2,'z0'=2,'co'=2,'xl'=2,'y1'=2,'y0'=2] {'co'}, dimensions={0}, use_global_device_ids=true | all-gather | bytes 196608 | tf_op jit(solution)/shard_map/all_gather | solution.py:72
  36.1 0.0 all-to-all-done
  36.2 0.4 fusion.10
  36.6 0.0 copy-start
  36.6 0.5 fusion.38
  37.1 2.3 %fusion = (f32[512]{0:T(512)S(1)}, f32[512]{0:T(512)S(1)}, f32[1024]{0:T(1024)S(1)}, f32[1024]{0:T(1024)S(1)}, f32[512,1024]{1,0:T(8,128)}) fusion(f32[512,1024]{1,0:T(8,128)S(1)} %get-tuple-element.34, f32[512]{0:T(512)S(1)} %get-tuple-element.16, f32[512,1024]{1,0:T(8,128)S(1)} %fusion.10, f32[1024]{0:T(1024)S(1)} %get-tuple-element.17, ...), kind=kOutput, calls=%fused_computation.7 | convolution fusion | flops 71300096 | bytes 6572032 | tf_op jit(solution)/shard_map/dot_general | solution.py:31
  39.4 0.0 copy-done
  39.5 0.7 broadcast_in_dim.8
  40.2 5.2 %all-to-all-start.1 = ((f32[16,3,1024]{2,1,0:T(4,128)}), f32[16,3,1024]{2,1,0:T(4,128)S(1)}, u32[]{:S(2)}, u32[]{:S(2)}) async-start(f32[16,3,1024]{2,1,0:T(4,128)} %broadcast_in_dim.8), calls=%async_computation.1 | async-start | bytes 524288 | tf_op jit(solution)/shard_map/all_to_all | solution.py:81
  45.4 2.4 %all-gather.2 = f32[2,3,512]{2,1,0:T(4,128)S(1)} all-gather(f32[1,3,512]{2,1,0:T(4,128)S(1)} %maximum_bitcast_fusion.1), channel_id=2, replica_groups=mesh['xh'=2,'z3'=2,'z2'=2,'z1'=2,'z0'=2,'co'=2,'xl'=2,'y1'=2,'y0'=2] {'co'}, dimensions={0}, use_global_device_ids=true | all-gather | bytes 18432 | tf_op jit(solution)/shard_map/all_gather | solution.py:84
  47.8 0.6 fusion.6
  48.4 1.7 %all-to-all-done.1 = f32[16,3,1024]{2,1,0:T(4,128)S(1)} async-done(((f32[16,3,1024]{2,1,0:T(4,128)}), f32[16,3,1024]{2,1,0:T(4,128)S(1)}, u32[]{:S(2)}, u32[]{:S(2)}) %all-to-all-start.1) | async-done | bytes 196640 | tf_op jit(solution)/shard_map/all_to_all | solution.py:81
  50.1 0.2 fusion.39
  50.3 0.1 fusion.27
  50.3 3.3 %add_convert_fusion = bf16[512,1024]{1,0:T(8,128)(2,1)S(1)} fusion(f32[512,1024]{1,0:T(8,128)} %copy-done, f32[512,1024]{1,0:T(8,128)} %get-tuple-element.35, f32[1024]{0:T(1024)S(1)} %div.35, f32[512]{0:T(512)S(1)} %div.32, f32[1024]{0:T(1024)S(1)} %get-tuple-element.18, f32[512,1024]{1,0:T(8,128)S(1)} %get-tuple-element.34, f32[1024]{0:T(1024)S(1)} %get-tuple-element.23, ...), kind=kLoop, calls=%fused_computation | loop fusion | flops 5242880 | bytes 7358464 | tf_op jit(solution)/shard_map/convert_element_type | solution.py:91
  53.6 0.4 convolution_multiply_fusion.2
  54.0 0.5 fusion.5
  54.5 0.3 fusion.4
  54.9 0.7 copy.65
  55.5 8.2 %all-to-all-start.2 = ((bf16[32,16,128]{2,1,0:T(8,128)(2,1)}), bf16[32,16,128]{2,1,0:T(8,128)(2,1)S(1)}, u32[]{:S(2)}, u32[]{:S(2)}) async-start(bf16[32,16,128]{2,1,0:T(8,128)(2,1)} %bitcast.21), calls=%async_computation.2 | async-start | bytes 262144 | tf_op jit(solution)/shard_map/all_to_all | solution.py:106
  63.7 1.9 %all-gather.1 = bf16[128,512]{1,0:T(8,128)(2,1)S(1)} all-gather(bf16[64,512]{1,0:T(8,128)(2,1)S(1)} %fusion.5), channel_id=3, replica_groups=mesh['xh'=2,'z3'=2,'z2'=2,'z1'=2,'z0'=2,'co'=2,'xl'=2,'y1'=2,'y0'=2] {'co'}, dimensions={0}, use_global_device_ids=true | all-gather | bytes 196608 | tf_op jit(solution)/shard_map/all_gather | solution.py:99
  65.7 8.7 %collective-permute-start.1 = (bf16[64,256]{1,0:T(8,128)(2,1)S(1)}, bf16[64,256]{1,0:T(8,128)(2,1)S(1)}, u32[]{:S(2)}, u32[]{:S(2)}) collective-permute-start(bf16[64,256]{1,0:T(8,128)(2,1)S(1)} %fusion.31), channel_id=1, source_target_pairs={{3,0},{67,1},{131,2},{195,3},{259,4},{323,5},{387,6},{451,7},{35,8... | collective-permute-start | bytes 98312 | tf_op jit(solution)/shard_map/ppermute | solution.py:102
  74.3 5.3 %collective-permute-done.1 = bf16[64,256]{1,0:T(8,128)(2,1)S(1)} collective-permute-done((bf16[64,256]{1,0:T(8,128)(2,1)S(1)}, bf16[64,256]{1,0:T(8,128)(2,1)S(1)}, u32[]{:S(2)}, u32[]{:S(2)}) %collective-permute-start.1) | collective-permute-done | bytes 32800 | tf_op jit(solution)/shard_map/ppermute | solution.py:102
  79.6 4.2 %all_gather.27 = bf16[128,256]{1,0:T(8,128)(2,1)S(1)} all-gather(bf16[64,256]{1,0:T(8,128)(2,1)S(1)} %collective-permute-done.1), channel_id=1, replica_groups=mesh['xh'=2,'z3'=2,'z2'=2,'z1'=2,'z0'=2,'co'=2,'xl'=2,'y1'=2,'y0'=2] {'co'}, dimensions={0}, use_global_device_ids=true | all-gather | bytes 98304 | tf_op jit(solution)/shard_map/all_gather | solution.py:111
  83.8 0.7 copy.67
  84.5 0.0 all-to-all-done.2
  84.6 0.6 copy_bitcast_fusion.2
  (16 shorter events, 0.3 us)
Async XLA Ops:
  2.1 34.0 %all-to-all-start = ((bf16[32,32,128]{2,1,0:T(8,128)(2,1)}), bf16[32,32,128]{2,1,0:T(8,128)(2,1)S(1)}, u32[]{:S(2)}, u32[]{:S(2)}) async-start(bf16[32,32,128]{2,1,0:T(8,128)(2,1)} %bitcast.2), calls=%async_computation | async-start | bytes 524288 | tf_op jit(solution)/shard_map/all_to_all | solution.py:69
  14.5 18.1 %collective-permute-start = (bf16[256,128]{1,0:T(8,128)(2,1)S(1)}, bf16[256,128]{1,0:T(8,128)(2,1)S(1)}, u32[]{:S(2)}, u32[]{:S(2)}) collective-permute-start(bf16[256,128]{1,0:T(8,128)(2,1)S(1)} %pad_maximum_fusion.1), channel_id=1, source_target_pairs={{0,3},{1,67},{2,131},{3,195},{4,259},{5,323},{6,387},{7,451},{8,35... | collective-permute-start | bytes 196616 | tf_op jit(solution)/shard_map/ppermute | solution.py:64
  36.6 2.8 %copy-start = (f32[512,1024]{1,0:T(8,128)}, f32[512,1024]{1,0:T(8,128)S(1)}, u32[]{:S(2)}) copy-start(f32[512,1024]{1,0:T(8,128)S(1)} %fusion.10) | copy-start | bytes 6291460
  40.2 9.9 %all-to-all-start.1 = ((f32[16,3,1024]{2,1,0:T(4,128)}), f32[16,3,1024]{2,1,0:T(4,128)S(1)}, u32[]{:S(2)}, u32[]{:S(2)}) async-start(f32[16,3,1024]{2,1,0:T(4,128)} %broadcast_in_dim.8), calls=%async_computation.1 | async-start | bytes 524288 | tf_op jit(solution)/shard_map/all_to_all | solution.py:81
  55.5 29.0 %all-to-all-start.2 = ((bf16[32,16,128]{2,1,0:T(8,128)(2,1)}), bf16[32,16,128]{2,1,0:T(8,128)(2,1)S(1)}, u32[]{:S(2)}, u32[]{:S(2)}) async-start(bf16[32,16,128]{2,1,0:T(8,128)(2,1)} %bitcast.21), calls=%async_computation.2 | async-start | bytes 262144 | tf_op jit(solution)/shard_map/all_to_all | solution.py:106
  65.7 14.0 %collective-permute-start.1 = (bf16[64,256]{1,0:T(8,128)(2,1)S(1)}, bf16[64,256]{1,0:T(8,128)(2,1)S(1)}, u32[]{:S(2)}, u32[]{:S(2)}) collective-permute-start(bf16[64,256]{1,0:T(8,128)(2,1)S(1)} %fusion.31), channel_id=1, source_target_pairs={{3,0},{67,1},{131,2},{195,3},{259,4},{323,5},{387,6},{451,7},{35,8... | collective-permute-start | bytes 98312 | tf_op jit(solution)/shard_map/ppermute | solution.py:102

commit v3 on v2

--- a/solution.py
+++ b/solution.py
@@ -21,7 +21,7 @@
     for source in range(512):
         xh, z3, z2, z1, z0, co, xl, y1, y0 = ((source >> k) & 1 for k in range(8, -1, -1))
         target = 0
-        for bit in (xl, y1, y0, co, z0, z1, xh, 1 - z3, 1 - z2):
+        for bit in (xl, y1, y0, co, z0 ^ z1 ^ co ^ 1, z1, xh, 1 - z3, 1 - z2):
             target = 2 * target + bit
         pairs.append((source, target))
     return pairs
@@ -34,20 +34,16 @@
 def moments(scores, moment, dim):
     highest = jnp.max(scores, axis=dim, keepdims=True)
     scaled = jnp.exp(scores - highest)
-    return jnp.stack(
-        (
-            highest.reshape(-1),
-            jnp.sum(scaled, axis=dim),
-            jnp.sum(scaled * moment, axis=dim),
-        )
-    )
+    sums = (jnp.sum(scaled, axis=dim), jnp.sum(scaled * moment, axis=dim))
+    return jnp.stack((highest.reshape(-1), *sums)), scaled
 
 
-def totals(parts):
+def totals(parts, own):
     highest = jnp.max(parts[:, 0], axis=0)
     factor = jnp.exp(parts[:, 0] - highest)
     total = jnp.sum(parts[:, 1] * factor, axis=0)
-    return highest, total, jnp.sum(parts[:, 2] * factor, axis=0) / total
+    delta = jnp.sum(parts[:, 2] * factor, axis=0) / total
+    return jnp.exp(own[0] - highest) / total, delta
 
 
 def shards(spec_emb, img_emb, grad_spec, grad_img):
@@ -76,20 +72,19 @@
     scores = dot(spec_rows, image_rows, across) * SCALE
     row_moment = dot(spec_grad, image_rows, across)
     column_moment = dot(spec_rows, image_grad, across)
-    column_part = moments(scores, column_moment, 0)
-    row_part = moments(scores, row_moment, 1)
+    column_part, column_scaled = moments(scores, column_moment, 0)
+    row_part, row_scaled = moments(scores, row_moment, 1)
     column_parts = lax.all_to_all(
         jnp.broadcast_to(column_part, (16, *column_part.shape)), ROWS, 0, 0, tiled=True
     )
     row_parts = lax.all_gather(row_part, "co")
-    row_high, row_total, row_delta = (t[:, None] for t in totals(row_parts))
-    column_high, column_total, column_delta = (t[None, :] for t in totals(column_parts))
-    row_weight = jnp.exp(scores - row_high) / row_total
-    column_weight = jnp.exp(scores - column_high) / column_total
-    slope = (
-        row_weight * (row_moment - row_delta) + column_weight * (column_moment - column_delta)
-    ).astype(jnp.bfloat16)
-    row_weight = row_weight.astype(jnp.bfloat16)
+    row_factor, row_delta = (t[:, None] for t in totals(row_parts, row_part))
+    row_weight = row_scaled * row_factor
+    row_slope = row_weight * (row_moment - row_delta)
+    row_weight, row_slope = lax.optimization_barrier((row_weight.astype(jnp.bfloat16), row_slope))
+    column_factor, column_delta = (t[None, :] for t in totals(column_parts, column_part))
+    column_weight = column_scaled * column_factor
+    slope = (row_slope + column_weight * (column_moment - column_delta)).astype(jnp.bfloat16)
     column_weight = column_weight.astype(jnp.bfloat16)
     last = ((1,), (1,))
     spec_part = SCALE * dot(image_rows, slope, last) + dot(image_grad, column_weight, last)

time: 85.7 us -> 87.1 us (1.016)
  other arithmetic: 5.32 us -> 8.58 us
  starting transfers between devices: 44.7 us -> 43.4 us
    mul x0 -> x1, other arithmetic: none -> 3.51 us  [shards(): row_slope = row_weight * (row_moment - row_delta)]
    all_to_all x1, starting transfers between devices: 8.16 us -> 6.81 us  [shards(): image_parts = lax.all_to_all(image_part, GROUP, 0, 0, tiled=True)]
    all_gather x1, blocking collectives: 1.9 us -> 3.25 us  [shards(): spec_parts = lax.all_gather(spec_part.astype(jnp.bfloat16), 'co')]
    all_gather x1, blocking collectives: 4.18 us -> 3.16 us  [shards(): spec_heads = lax.all_gather(spec_back, 'co', tiled=True)]
    ppermute x1, waiting for transfers between devices: 5.3 us -> 6.22 us  [shards(): spec_back = lax.ppermute(spec_sum, EVERY, [(b, a) for a, b in moves])]
    all_to_all x1, waiting for transfers between devices: 1.66 us -> 0.79 us  [shards(): lax.all_to_all(jnp.broadcast_to(column_part, (16, *column_part.shape)), R...]
  transfers between devices with their start and end apart: 5 -> 5, of which waited for: 3 -> 3; matrix products, arithmetic and copies ran while one was open for 3% -> 7% of each run, Pallas kernels for 0% -> 0%
where the time goes in v3:
time: 87.1 us; the launch traced here: 86.5 us
  starting transfers between devices  43.4 us (50%)
  blocking collectives  13 us (15%)
  waiting for transfers between devices  12 us (14%)
  other arithmetic  8.58 us (10%)
  matrix products  5.16 us (6%)
  local copies, waits for them, and re-layouts  3.61 us (4%)
    ppermute x1, starting transfers between devices, shards(): own = lax.ppermute(own, EVERY, moves)  13.2 us
    all_to_all x1, starting transfers between devices, shards(): image = lax.all_to_all(image, GROUP, 0, 0, tiled=True)  9.54 us
    ppermute x1, starting transfers between devices, shards(): spec_back = lax.ppermute(spec_sum, EVERY, [(b, a) for a, b in moves])  7.86 us
    all_to_all x1, starting transfers between devices, shards(): image_parts = lax.all_to_all(image_part, GROUP, 0, 0, tiled=True)  6.81 us
    ppermute x1, waiting for transfers between devices, shards(): spec_back = lax.ppermute(spec_sum, EVERY, [(b, a) for a, b in moves])  6.22 us
    all_to_all x1, starting transfers between devices, shards(): lax.all_to_all(jnp.broadcast_to(column_part, (16, *column_part.shape)), R...  6 us
    dot_general x7, matrix products, dot(): lax.dot_general(a, b, (dims, ((), ())), preferred_element_type=jnp.float32)  5.16 us
    ppermute x1, waiting for transfers between devices, shards(): own = lax.ppermute(own, EVERY, moves)  5.01 us
  transfers between devices with their start and end apart: 5, of which 3 were waited for; matrix products, arithmetic and copies ran while one was open for 7% of the time, Pallas kernels for 0%

profile of v3, /device:TPU:19, one launch (start us, length us, event | category | flops | bytes accessed | tf_op | source)
XLA Modules:
  0.0 86.5 jit_solution(8843983311252834175)
XLA Ops:
  0.6 0.7 maximum_bitcast_fusion
  1.4 0.7 broadcast_in_dim.4
  2.1 9.5 %all-to-all-start = ((bf16[32,32,128]{2,1,0:T(8,128)(2,1)}), bf16[32,32,128]{2,1,0:T(8,128)(2,1)S(1)}, u32[]{:S(2)}, u32[]{:S(2)}) async-start(bf16[32,32,128]{2,1,0:T(8,128)(2,1)} %bitcast.2), calls=%async_computation | async-start | bytes 524288 | tf_op jit(solution)/shard_map/all_to_all | solution.py:65
  11.7 0.8 pad_maximum_fusion
  12.4 1.9 %all_gather.21 = bf16[256,256]{1,0:T(8,128)(2,1)S(1)} all-gather(bf16[128,256]{1,0:T(8,128)(2,1)S(1)} %pad_maximum_fusion), channel_id=1, replica_groups=mesh['xh'=2,'z3'=2,'z2'=2,'z1'=2,'z0'=2,'co'=2,'xl'=2,'y1'=2,'y0'=2] {'co'}, dimensions={0}, use_global_device_ids=true | all-gather | bytes 196608 | tf_op jit(solution)/shard_map/all_gather | solution.py:55
  14.3 0.1 slice_select_fusion.2
  14.5 0.1 pad_maximum_fusion.1
  14.5 13.2 %collective-permute-start = (bf16[256,128]{1,0:T(8,128)(2,1)S(1)}, bf16[256,128]{1,0:T(8,128)(2,1)S(1)}, u32[]{:S(2)}, u32[]{:S(2)}) collective-permute-start(bf16[256,128]{1,0:T(8,128)(2,1)S(1)} %pad_maximum_fusion.1), channel_id=1, source_target_pairs={{0,19},{1,83},{2,147},{3,211},{4,275},{5,339},{6,403},{7,467},{8,3... | collective-permute-start | bytes 196616 | tf_op jit(solution)/shard_map/ppermute | solution.py:60
  27.7 5.0 %collective-permute-done = bf16[256,128]{1,0:T(8,128)(2,1)S(1)} collective-permute-done((bf16[256,128]{1,0:T(8,128)(2,1)S(1)}, bf16[256,128]{1,0:T(8,128)(2,1)S(1)}, u32[]{:S(2)}, u32[]{:S(2)}) %collective-permute-start) | collective-permute-done | bytes 65568 | tf_op jit(solution)/shard_map/ppermute | solution.py:60
  32.7 2.8 %all_gather.22 = bf16[512,128]{1,0:T(8,128)(2,1)S(1)} all-gather(bf16[256,128]{1,0:T(8,128)(2,1)S(1)} %collective-permute-done), channel_id=1, replica_groups=mesh['xh'=2,'z3'=2,'z2'=2,'z1'=2,'z0'=2,'co'=2,'xl'=2,'y1'=2,'y0'=2] {'co'}, dimensions={0}, use_global_device_ids=true | all-gather | bytes 196608 | tf_op jit(solution)/shard_map/all_gather | solution.py:68
  35.6 0.0 all-to-all-done
  35.6 0.5 fusion.10
  36.1 0.0 copy-start
  36.1 0.5 multiply_reduce_fusion.2
  36.7 2.5 %fusion.5 = (f32[1024]{0:T(1024)S(1)}, f32[1024]{0:T(1024)S(1)}, f32[512]{0:T(512)S(1)}, f32[512]{0:T(512)S(1)}, f32[512,1024]{1,0:T(8,128)}) fusion(f32[1024]{0:T(1024)S(1)} %get-tuple-element.20, f32[512,1024]{1,0:T(8,128)S(1)} %get-tuple-element.44, f32[512,1024]{1,0:T(8,128)S(1)} %fusion.10, f32[512]{0:T(512)S(1)} %get-tuple-element.21, ...), kind=kOutput, calls=%fused_computation.18 | convolution fusion | flops 71824384 | bytes 6572032 | tf_op jit(solution)/shard_map/dot_general | solution.py:31
  39.1 0.0 copy-done
  39.2 1.8 %all-gather.2 = f32[2,3,512]{2,1,0:T(4,128)S(1)} all-gather(f32[1,3,512]{2,1,0:T(4,128)S(1)} %maximum_bitcast_fusion.1), channel_id=2, replica_groups=mesh['xh'=2,'z3'=2,'z2'=2,'z1'=2,'z0'=2,'co'=2,'xl'=2,'y1'=2,'y0'=2] {'co'}, dimensions={0}, use_global_device_ids=true | all-gather | bytes 18432 | tf_op jit(solution)/shard_map/all_gather | solution.py:80
  41.0 0.8 broadcast_in_dim.5
  41.8 6.0 %all-to-all-start.1 = ((f32[16,3,1024]{2,1,0:T(4,128)}), f32[16,3,1024]{2,1,0:T(4,128)S(1)}, u32[]{:S(2)}, u32[]{:S(2)}) async-start(f32[16,3,1024]{2,1,0:T(4,128)} %broadcast_in_dim.5), calls=%async_computation.1 | async-start | bytes 524288 | tf_op jit(solution)/shard_map/all_to_all | solution.py:77
  47.8 3.5 %subtract_multiply_fusion = (f32[512,1024]{1,0:T(8,128)}, bf16[512,1024]{1,0:T(8,128)(2,1)S(1)}) fusion(f32[512,1024]{1,0:T(8,128)} %copy-done, f32[512]{0:T(512)S(1)} %get-tuple-element.42, f32[512]{0:T(512)S(1)} %get-tuple-element.43, f32[512]{0:T(512)S(1)} %get-tuple-element.21, f32[512,1024]{1,0:T(8,128)S(1)} %get-tuple-element.44), kind=kLoop, calls=%fused_computation.3 | loop fusion | flops 3145728 | bytes 7346176 | tf_op jit(solution)/shard_map/mul | solution.py:83
  51.4 0.4 fusion.16
  51.8 0.8 all-to-all-done.1
  52.5 0.2 fusion.39
  52.7 0.1 fusion.26
  52.8 3.0 %add_convert_fusion = bf16[512,1024]{1,0:T(8,128)(2,1)S(1)} fusion(f32[512,1024]{1,0:T(8,128)} %get-tuple-element.4, f32[512,1024]{1,0:T(8,128)} %get-tuple-element.45, f32[1024]{0:T(1024)S(1)} %get-tuple-element.41, f32[1024]{0:T(1024)S(1)} %get-tuple-element.40, f32[1024]{0:T(1024)S(1)} %get-tuple-element.20, f32[512,1024]{1,0:T(8,128)S(1)} %get-tuple-element.44), kind=kLoop, calls=%fused_computation | loop fusion | flops 3670016 | bytes 7352320 | tf_op jit(solution)/shard_map/convert_element_type | solution.py:87
  55.8 0.4 convolution_multiply_fusion.1
  56.2 0.6 fusion.3
  56.8 3.2 %all-gather.1 = bf16[128,512]{1,0:T(8,128)(2,1)S(1)} all-gather(bf16[64,512]{1,0:T(8,128)(2,1)S(1)} %fusion.3), channel_id=3, replica_groups=mesh['xh'=2,'z3'=2,'z2'=2,'z1'=2,'z0'=2,'co'=2,'xl'=2,'y1'=2,'y0'=2] {'co'}, dimensions={0}, use_global_device_ids=true | all-gather | bytes 196608 | tf_op jit(solution)/shard_map/all_gather | solution.py:94
  60.0 0.3 fusion.2
  60.4 0.7 copy.65
  61.0 6.8 %all-to-all-start.2 = ((bf16[32,16,128]{2,1,0:T(8,128)(2,1)}), bf16[32,16,128]{2,1,0:T(8,128)(2,1)S(1)}, u32[]{:S(2)}, u32[]{:S(2)}) async-start(bf16[32,16,128]{2,1,0:T(8,128)(2,1)} %bitcast.21), calls=%async_computation.2 | async-start | bytes 262144 | tf_op jit(solution)/shard_map/all_to_all | solution.py:101
  67.9 7.9 %collective-permute-start.1 = (bf16[64,256]{1,0:T(8,128)(2,1)S(1)}, bf16[64,256]{1,0:T(8,128)(2,1)S(1)}, u32[]{:S(2)}, u32[]{:S(2)}) collective-permute-start(bf16[64,256]{1,0:T(8,128)(2,1)S(1)} %fusion.30), channel_id=1, source_target_pairs={{19,0},{83,1},{147,2},{211,3},{275,4},{339,5},{403,6},{467,7},{35,... | collective-permute-start | bytes 98312 | tf_op jit(solution)/shard_map/ppermute | solution.py:97
  75.8 6.2 %collective-permute-done.1 = bf16[64,256]{1,0:T(8,128)(2,1)S(1)} collective-permute-done((bf16[64,256]{1,0:T(8,128)(2,1)S(1)}, bf16[64,256]{1,0:T(8,128)(2,1)S(1)}, u32[]{:S(2)}, u32[]{:S(2)}) %collective-permute-start.1) | collective-permute-done | bytes 32800 | tf_op jit(solution)/shard_map/ppermute | solution.py:97
  82.0 3.2 %all_gather.27 = bf16[128,256]{1,0:T(8,128)(2,1)S(1)} all-gather(bf16[64,256]{1,0:T(8,128)(2,1)S(1)} %collective-permute-done.1), channel_id=1, replica_groups=mesh['xh'=2,'z3'=2,'z2'=2,'z1'=2,'z0'=2,'co'=2,'xl'=2,'y1'=2,'y0'=2] {'co'}, dimensions={0}, use_global_device_ids=true | all-gather | bytes 98304 | tf_op jit(solution)/shard_map/all_gather | solution.py:106
  85.2 0.7 copy.67
  85.9 0.0 all-to-all-done.2
  85.9 0.6 copy_bitcast_fusion.2
  (16 shorter events, 0.3 us)
Async XLA Ops:
  2.1 33.5 %all-to-all-start = ((bf16[32,32,128]{2,1,0:T(8,128)(2,1)}), bf16[32,32,128]{2,1,0:T(8,128)(2,1)S(1)}, u32[]{:S(2)}, u32[]{:S(2)}) async-start(bf16[32,32,128]{2,1,0:T(8,128)(2,1)} %bitcast.2), calls=%async_computation | async-start | bytes 524288 | tf_op jit(solution)/shard_map/all_to_all | solution.py:65
  14.5 18.2 %collective-permute-start = (bf16[256,128]{1,0:T(8,128)(2,1)S(1)}, bf16[256,128]{1,0:T(8,128)(2,1)S(1)}, u32[]{:S(2)}, u32[]{:S(2)}) collective-permute-start(bf16[256,128]{1,0:T(8,128)(2,1)S(1)} %pad_maximum_fusion.1), channel_id=1, source_target_pairs={{0,19},{1,83},{2,147},{3,211},{4,275},{5,339},{6,403},{7,467},{8,3... | collective-permute-start | bytes 196616 | tf_op jit(solution)/shard_map/ppermute | solution.py:60
  36.1 3.0 %copy-start = (f32[512,1024]{1,0:T(8,128)}, f32[512,1024]{1,0:T(8,128)S(1)}, u32[]{:S(2)}) copy-start(f32[512,1024]{1,0:T(8,128)S(1)} %fusion.10) | copy-start | bytes 6291460
  41.8 10.7 %all-to-all-start.1 = ((f32[16,3,1024]{2,1,0:T(4,128)}), f32[16,3,1024]{2,1,0:T(4,128)S(1)}, u32[]{:S(2)}, u32[]{:S(2)}) async-start(f32[16,3,1024]{2,1,0:T(4,128)} %broadcast_in_dim.5), calls=%async_computation.1 | async-start | bytes 524288 | tf_op jit(solution)/shard_map/all_to_all | solution.py:77
  61.0 24.8 %all-to-all-start.2 = ((bf16[32,16,128]{2,1,0:T(8,128)(2,1)}), bf16[32,16,128]{2,1,0:T(8,128)(2,1)S(1)}, u32[]{:S(2)}, u32[]{:S(2)}) async-start(bf16[32,16,128]{2,1,0:T(8,128)(2,1)} %bitcast.21), calls=%async_computation.2 | async-start | bytes 262144 | tf_op jit(solution)/shard_map/all_to_all | solution.py:101
  67.9 14.1 %collective-permute-start.1 = (bf16[64,256]{1,0:T(8,128)(2,1)S(1)}, bf16[64,256]{1,0:T(8,128)(2,1)S(1)}, u32[]{:S(2)}, u32[]{:S(2)}) collective-permute-start(bf16[64,256]{1,0:T(8,128)(2,1)S(1)} %fusion.30), channel_id=1, source_target_pairs={{19,0},{83,1},{147,2},{211,3},{275,4},{339,5},{403,6},{467,7},{35,... | collective-permute-start | bytes 98312 | tf_op jit(solution)/shard_map/ppermute | solution.py:97

commit v4 on v3

v4 whole, which is shorter than its diff:
```python
import jax
import jax.numpy as jnp
from jax import lax
from jax.experimental import pallas as pl
from jax.experimental.pallas import tpu as pltpu
from jax.sharding import Mesh
from jax.sharding import PartitionSpec as P


D = 1024
HEADS = 16
SIZE = D // HEADS
SPEC = ("xh", "z3", "z2", "z1", "z0", "co")
IMG = ("xl", "y1", "y0")
EVERY = SPEC + IMG
GROUP = ("z0", "co", "xl", "y1", "y0")
ROWS = ("z0", "xl", "y1", "y0")
SCALE = SIZE**-0.5


def head_moves():
    pairs = []
    for source in range(512):
        xh, z3, z2, z1, z0, co, xl, y1, y0 = ((source >> k) & 1 for k in range(8, -1, -1))
        target = 0
        for bit in (xl, y1, y0, co, z0 ^ z1 ^ co ^ 1, z1, xh, 1 - z3, 1 - z2):
            target = 2 * target + bit
        pairs.append((source, target))
    return pairs


def dot(a, b, dims):
    return lax.dot_general(a, b, (dims, ((), ())), preferred_element_type=jnp.float32)


BLOCK = 128
CHUNK = 16
LANES = 128


def row_blocks(total, size):
    return [slice(k, k + size) for k in range(0, total, size)]


def unpack(pieces, image):
    groups = image.shape[1] // LANES
    size = SIZE // 4
    for f in range(4):
        for k in range(groups):
            for kind in range(2):
                image[kind * SIZE + f * size : kind * SIZE + (f + 1) * size, k * LANES : (k + 1) * LANES] = (
                    pieces[f * groups + k, kind * size : (kind + 1) * size, :]
                )


def stats_kernel(both, pieces, column_out, row_out, z_ref, p_ref, q_ref, image):
    rows, tokens = z_ref.shape
    unpack(pieces, image)
    peak = None
    for block in row_blocks(rows, BLOCK):
        z = dot(both[block, :SIZE], image[:SIZE, :], ((1,), (0,))) * SCALE
        z_ref[block, :] = z
        q_ref[block, :] = dot(both[block, :SIZE], image[SIZE:, :], ((1,), (0,)))
        p_ref[block, :] = dot(both[block, SIZE:], image[:SIZE, :], ((1,), (0,)))
        for part in row_blocks(BLOCK, 8):
            peak = z[part] if peak is None else jnp.maximum(peak, z[part])
    high = jnp.max(peak, axis=0, keepdims=True)
    total = jnp.zeros((8, tokens), jnp.float32)
    weighted = jnp.zeros((8, tokens), jnp.float32)
    lane = lax.broadcasted_iota(jnp.int32, (8, LANES), 1)
    columns = []
    for part in row_blocks(rows, 8):
        z = z_ref[part, :]
        scaled = jnp.exp(z - high)
        total = total + scaled
        weighted = weighted + scaled * q_ref[part, :]
        row_high = jnp.max(z, axis=1, keepdims=True)
        scaled = jnp.exp(z - row_high)
        row_total = jnp.sum(scaled, axis=1, keepdims=True)
        row_weighted = jnp.sum(scaled * p_ref[part, :], axis=1, keepdims=True)
        columns.append(jnp.where(lane == 0, row_high, jnp.where(lane == 1, row_total, row_weighted)))
        if len(columns) * 8 == LANES:
            base = part.stop - LANES
            row_out[:, base : base + LANES] = jnp.concatenate(columns, axis=0).T[:8]
            columns = []
    sums = (
        high,
        jnp.sum(total, axis=0, keepdims=True),
        jnp.sum(weighted, axis=0, keepdims=True),
    )
    piece = jnp.concatenate([v[:, k] for v in sums for k in row_blocks(tokens, LANES)], axis=0)
    for peer in range(column_out.shape[0]):
        column_out[peer] = piece


def slope_kernel(
    both,
    turned,
    pieces,
    row_ref,
    column_ref,
    spec_out,
    image_out,
    z_ref,
    p_ref,
    q_ref,
    s_ref,
    r_ref,
    c_ref,
    image,
):
    rows, tokens = z_ref.shape
    unpack(pieces, image)
    groups = tokens // LANES
    across = ((1,), (0,))
    peers = column_ref.shape[0]
    high = column_ref[0, :groups]
    for peer in range(1, peers):
        high = jnp.maximum(high, column_ref[peer, :groups])
    total = weighted = 0.0
    for peer in range(peers):
        factor = jnp.exp(column_ref[peer, :groups] - high)
        total = total + column_ref[peer, groups : 2 * groups] * factor
        weighted = weighted + column_ref[peer, 2 * groups :] * factor
    shrink = 1.0 / total
    delta = weighted * shrink

    def products(block):
        z_ref[block, :] = dot(both[block, :SIZE], image[:SIZE, :], across) * SCALE
        p_ref[block, :] = dot(both[block, SIZE:], image[:SIZE, :], across)
        q_ref[block, :] = dot(both[block, :SIZE], image[SIZE:, :], across)

    blocks = row_blocks(rows, BLOCK)
    products(blocks[0])
    for n, block in enumerate(blocks):
        if n + 1 < len(blocks):
            products(blocks[n + 1])
        for part in row_blocks(BLOCK, CHUNK):
            part = slice(block.start + part.start, block.start + part.stop)
            row_high = jnp.broadcast_to(row_ref[part, 0:1], (CHUNK, LANES))
            row_shrink = jnp.broadcast_to(row_ref[part, 1:2], (CHUNK, LANES))
            row_delta = jnp.broadcast_to(row_ref[part, 2:3], (CHUNK, LANES))
            for k in range(groups):
                place = slice(k * LANES, (k + 1) * LANES)
                z = z_ref[part, place]
                row = jnp.exp(z - row_high) * row_shrink
                column = jnp.exp(z - high[k : k + 1]) * shrink[k : k + 1]
                slope = row * (p_ref[part, place] - row_delta) + column * (
                    q_ref[part, place] - delta[k : k + 1]
                )
                s_ref[part, place] = slope.astype(jnp.bfloat16)
                r_ref[part, place] = row.astype(jnp.bfloat16)
                c_ref[part, place] = column.astype(jnp.bfloat16)
        last = ((1,), (1,))
        spec_out[:, block] = (
            SCALE * dot(image[:SIZE, :], s_ref[block, :], last) + dot(image[SIZE:, :], c_ref[block, :], last)
        ).astype(jnp.bfloat16)
    image_part = SCALE * dot(turned[:SIZE, :], s_ref[...], across) + dot(turned[SIZE:, :], r_ref[...], across)
    image_part = image_part.astype(jnp.bfloat16)
    size = SIZE // 4
    for f in range(4):
        for k in range(groups):
            image_out[f * groups + k] = image_part[f * size : (f + 1) * size, k * LANES : (k + 1) * LANES]


def statistics(both, image, peers):
    rows, tokens = both.shape[0], image.shape[0] // 4 * LANES
    wide = pltpu.VMEM((rows, tokens), jnp.float32)
    return pl.pallas_call(
        stats_kernel,
        out_shape=(
            jax.ShapeDtypeStruct((peers, 3 * tokens // LANES, LANES), jnp.float32),
            jax.ShapeDtypeStruct((8, rows), jnp.float32),
        ),
        scratch_shapes=[wide, wide, wide, pltpu.VMEM((2 * SIZE, tokens), jnp.bfloat16)],
    )(both, image)


def gradients(both, turned, image, row_stats, column_parts):
    rows, tokens = both.shape[0], image.shape[0] // 4 * LANES
    wide = pltpu.VMEM((rows, tokens), jnp.float32)
    narrow = pltpu.VMEM((rows, tokens), jnp.bfloat16)
    return pl.pallas_call(
        slope_kernel,
        out_shape=(
            jax.ShapeDtypeStruct((SIZE, rows), jnp.bfloat16),
            jax.ShapeDtypeStruct((4 * tokens // LANES, SIZE // 4, LANES), jnp.bfloat16),
        ),
        scratch_shapes=[
            *(wide, wide, wide, narrow, narrow, narrow),
            pltpu.VMEM((2 * SIZE, tokens), jnp.bfloat16),
        ],
    )(both, turned, image, row_stats, column_parts)


def row_totals(parts):
    highest = jnp.max(parts[:, 0], axis=0)
    factor = jnp.exp(parts[:, 0] - highest)
    total = jnp.sum(parts[:, 1] * factor, axis=0)
    delta = jnp.sum(parts[:, 2] * factor, axis=0) / total
    return jnp.stack((highest, 1.0 / total, delta), axis=1)


def shards(spec_emb, img_emb, grad_spec, grad_img):
    moves = head_moves()
    tokens = img_emb.shape[0]
    half = tokens // 2
    rows = spec_emb.shape[0]
    second = lax.axis_index("co") == 1
    own = lax.all_gather(jnp.concatenate([spec_emb, grad_spec], axis=1), "co", tiled=True)
    own = jnp.concatenate(
        [jnp.where(second, a[:, SIZE:], a[:, :SIZE]) for a in (own[:, : 2 * SIZE], own[:, 2 * SIZE :])],
        axis=1,
    )
    own = lax.ppermute(own, EVERY, moves)
    features = 2 * img_emb.shape[1]
    image = jnp.concatenate([img_emb, grad_img], axis=1).T.reshape(features, 2, half)
    image = jnp.moveaxis(image, 1, 0)[None, :, None]
    image = jnp.broadcast_to(image, (2, 2, 8, features, half)).reshape(32, features, half)
    image = lax.all_to_all(image, GROUP, 0, 0, tiled=True)
    both = lax.all_gather(own, "co", tiled=True)
    column_part, row_part = statistics(both, image, 16)
    column_parts = lax.all_to_all(column_part, ROWS, 0, 0, tiled=True)
    row_parts = lax.all_gather(row_part, "co")
    row_stats = row_totals(row_parts)
    spec_part, image_part = gradients(both, both.T, image, row_stats, column_parts)
    spec_parts = lax.all_gather(spec_part, "co")
    spec_parts = jnp.where(second, spec_parts[:, :, 2 * rows :], spec_parts[:, :, : 2 * rows])
    spec_sum = (spec_parts[0].astype(jnp.float32) + spec_parts[1]).astype(jnp.bfloat16)
    spec_back = lax.ppermute(spec_sum, EVERY, [(b, a) for a, b in moves])

    image_parts = lax.all_to_all(image_part, GROUP, 0, 0, tiled=True)
    image_parts = image_parts.reshape(2, 2, 8, SIZE // 4, half).astype(jnp.float32)
    image_sum = jnp.sum(image_parts, axis=(0, 2)).astype(jnp.bfloat16)
    image_result = jnp.moveaxis(image_sum, 1, 2).reshape(tokens, SIZE // 4)

    spec_heads = lax.all_gather(spec_back, "co", tiled=True)
    spec_result = jnp.where(second, spec_heads[:, rows:], spec_heads[:, :rows]).T
    return (spec_result, image_result)


def solution(mesh):
    split = Mesh(mesh.devices.reshape((2,) * 9), EVERY)

    return jax.shard_map(
        shards,
        mesh=split,
        in_specs=(P(SPEC, IMG), P(IMG, SPEC), P(SPEC, IMG), P(IMG, SPEC)),
        out_specs=(P(SPEC, IMG), P(IMG, SPEC)),
        check_vma=False,
    )
```

time: 87.1 us -> 85.8 us (0.985)
  Pallas kernels: 0 us -> 8.16 us
  other arithmetic: 8.58 us -> 0.86 us
  matrix products: 5.16 us -> 0 us
  local copies, waits for them, and re-layouts: 3.61 us -> 5.94 us
  starting transfers between devices: 43.4 us -> 44.9 us
    pallas_call x0 -> x2, Pallas kernels: none -> 8.16 us  [the longest x1 4.62 us: gradients(): pl.pallas_call(slope_kernel, out_shape=(jax.ShapeDtypeStruct((SIZE, rows)...]
    dot_general x7 -> x0, matrix products: 5.16 us -> none  [dot(): lax.dot_general(a, b, (dims, ((), ())), preferred_element_type=jnp.float32)]
    mul x1 -> x0, other arithmetic: 3.51 us -> none  [shards(): row_slope = row_weight * (row_moment - row_delta)]
    convert_element_type x1 -> x0, other arithmetic: 3 us -> none  [shards(): (row_slope + column_weight * (column_moment - column_delta)).astype(jnp.b...]
    unnamed x4 -> x17, local copies, waits for them, and re-layouts: 0.75 us -> 2.96 us
    all_gather x1, blocking collectives: 3.25 us -> 1.9 us  [shards(): spec_parts = lax.all_gather(spec_part, 'co')]
    all_to_all x1, starting transfers between devices: 6.81 us -> 8.11 us  [shards(): image_parts = lax.all_to_all(image_part, GROUP, 0, 0, tiled=True)]
  transfers between devices with their start and end apart: 5 -> 5, of which waited for: 3 -> 3; matrix products, arithmetic and copies ran while one was open for 7% -> 3% of each run, Pallas kernels for 0% -> 0%
where the time goes in v4:
time: 85.8 us; the launch traced here: 85 us
  starting transfers between devices  44.9 us (52%)
  blocking collectives  12.2 us (14%)
  waiting for transfers between devices  12.2 us (14%)
  Pallas kernels  8.16 us (10%)
  local copies, waits for them, and re-layouts  5.94 us (7%)
  other arithmetic  0.86 us (1%)
    ppermute x1, starting transfers between devices, shards(): own = lax.ppermute(own, EVERY, moves)  13.2 us
    all_to_all x1, starting transfers between devices, shards(): image = lax.all_to_all(image, GROUP, 0, 0, tiled=True)  9.67 us
    all_to_all x1, starting transfers between devices, shards(): image_parts = lax.all_to_all(image_part, GROUP, 0, 0, tiled=True)  8.11 us
    ppermute x1, starting transfers between devices, shards(): spec_back = lax.ppermute(spec_sum, EVERY, [(b, a) for a, b in moves])  7.82 us
    ppermute x1, waiting for transfers between devices, shards(): spec_back = lax.ppermute(spec_sum, EVERY, [(b, a) for a, b in moves])  6.26 us
    all_to_all x1, starting transfers between devices, shards(): column_parts = lax.all_to_all(column_part, ROWS, 0, 0, tiled=True)  6.14 us
    ppermute x1, waiting for transfers between devices, shards(): own = lax.ppermute(own, EVERY, moves)  5.01 us
    pallas_call x1, Pallas kernels, gradients(): pl.pallas_call(slope_kernel, out_shape=(jax.ShapeDtypeStruct((SIZE, rows)...  4.62 us
  transfers between devices with their start and end apart: 5, of which 3 were waited for; matrix products, arithmetic and copies ran while one was open for 3% of the time, Pallas kernels for 0%

profile of v4, /device:TPU:19, one launch (start us, length us, event | category | flops | bytes accessed | tf_op | source)
XLA Modules:
  0.0 85.0 jit_solution(13771380717192485174)
XLA Ops:
  0.6 0.7 maximum_bitcast_fusion
  1.4 0.7 broadcast_in_dim.2
  2.1 0.0 copy-start.4
  2.1 9.7 %all-to-all-start = ((bf16[32,32,128]{2,1,0:T(8,128)(2,1)}), bf16[32,32,128]{2,1,0:T(8,128)(2,1)S(1)}, u32[]{:S(2)}, u32[]{:S(2)}) async-start(bf16[32,32,128]{2,1,0:T(8,128)(2,1)} %bitcast.3), calls=%async_computation | async-start | bytes 524288 | tf_op jit(solution)/shard_map/all_to_all | solution.py:220
  11.8 0.0 copy-done.4
  11.8 0.0 copy-start.5
  11.8 0.1 copy.36
  11.9 0.6 copy-done.5
  12.6 0.1 copy.37
  12.7 1.9 %all_gather.21 = bf16[256,256]{0,1:T(8,128)(2,1)S(1)} all-gather(bf16[128,256]{0,1:T(8,128)(2,1)S(1)} %pad_maximum_fusion), channel_id=1, replica_groups=mesh['xh'=2,'z3'=2,'z2'=2,'z1'=2,'z0'=2,'co'=2,'xl'=2,'y1'=2,'y0'=2] {'co'}, dimensions={0}, use_global_device_ids=true | all-gather | bytes 196608 | tf_op jit(solution)/shard_map/all_gather | solution.py:210
  14.7 13.2 %collective-permute-start = (bf16[256,128]{0,1:T(8,128)(2,1)S(1)}, bf16[256,128]{0,1:T(8,128)(2,1)S(1)}, u32[]{:S(2)}, u32[]{:S(2)}) collective-permute-start(bf16[256,128]{0,1:T(8,128)(2,1)S(1)} %pad_maximum_fusion.1), channel_id=1, source_target_pairs={{0,19},{1,83},{2,147},{3,211},{4,275},{5,339},{6,403},{7,467},{8,3... | collective-permute-start | bytes 196616 | tf_op jit(solution)/shard_map/ppermute | solution.py:215
  27.8 5.0 %collective-permute-done = bf16[256,128]{0,1:T(8,128)(2,1)S(1)} collective-permute-done((bf16[256,128]{0,1:T(8,128)(2,1)S(1)}, bf16[256,128]{0,1:T(8,128)(2,1)S(1)}, u32[]{:S(2)}, u32[]{:S(2)}) %collective-permute-start) | collective-permute-done | bytes 65568 | tf_op jit(solution)/shard_map/ppermute | solution.py:215
  32.8 2.8 %all_gather.22 = bf16[512,128]{0,1:T(8,128)(2,1)S(1)} all-gather(bf16[256,128]{0,1:T(8,128)(2,1)S(1)} %collective-permute-done), channel_id=1, replica_groups=mesh['xh'=2,'z3'=2,'z2'=2,'z1'=2,'z0'=2,'co'=2,'xl'=2,'y1'=2,'y0'=2] {'co'}, dimensions={0}, use_global_device_ids=true | all-gather | bytes 196608 | tf_op jit(solution)/shard_map/all_gather | solution.py:221
  35.7 0.0 copy-start.1
  35.7 0.8 copy.42.both
  36.4 0.0 copy-done.1
  36.4 0.0 all-to-all-done.pieces
  36.4 0.0 copy-start
  36.4 0.7 copy-done
  37.1 3.5 %shard_map.59 = (f32[16,24,128]{2,1,0:T(8,128)}, f32[8,512]{1,0:T(8,128)}) custom-call(bf16[512,128]{1,0:T(8,128)(2,1)} %copy.42.both, bf16[32,32,128]{2,1,0:T(8,128)(2,1)} %copy-done), custom_call_target="tpu_custom_call" | custom-call | tf_op jit(solution)/shard_map/pallas_call | solution.py:169
  40.7 0.0 copy-start.6
  40.7 6.1 %all-to-all-start.1 = ((f32[16,24,128]{2,1,0:T(8,128)}), f32[16,24,128]{2,1,0:T(8,128)S(1)}, u32[]{:S(2)}, u32[]{:S(2)}) async-start(f32[16,24,128]{2,1,0:T(8,128)} %get-tuple-element.7), calls=%async_computation.1 | async-start | bytes 393216 | tf_op jit(solution)/shard_map/all_to_all | solution.py:223
  46.8 0.0 copy-done.6
  46.8 2.4 %all-gather = f32[16,512]{1,0:T(8,128)S(1)} all-gather(f32[8,512]{1,0:T(8,128)S(1)} %copy-done.6), channel_id=2, replica_groups=mesh['xh'=2,'z3'=2,'z2'=2,'z1'=2,'z0'=2,'co'=2,'xl'=2,'y1'=2,'y0'=2] {'co'}, dimensions={0}, use_global_device_ids=true | all-gather | bytes 49152 | tf_op jit(solution)/shard_map/all_gather | solution.py:224
  49.3 0.9 %copy.43.row_ref = f32[512,3]{1,0:T(8,128)} copy(f32[512,3]{0,1:T(4,128)S(1)} %pad_maximum_fusion.2) | data formatting | bytes 12288 | tf_op jit(solution)/shard_map/stack | solution.py:201
  50.2 0.9 %all-to-all-done.1.column_ref = f32[16,24,128]{2,1,0:T(8,128)S(1)} async-done(((f32[16,24,128]{2,1,0:T(8,128)}), f32[16,24,128]{2,1,0:T(8,128)S(1)}, u32[]{:S(2)}, u32[]{:S(2)}) %all-to-all-start.1) | async-done | bytes 196640 | tf_op jit(solution)/shard_map/all_to_all | solution.py:223
  51.1 0.0 copy-start.2
  51.1 0.7 copy-done.2
  51.7 4.6 %shard_map.60 = (bf16[64,512]{1,0:T(8,128)(2,1)}, bf16[32,16,128]{2,1,0:T(8,128)(2,1)}) custom-call(bf16[512,128]{1,0:T(8,128)(2,1)} %copy.42.both, bf16[128,512]{1,0:T(8,128)(2,1)} %bitcast.41, bf16[32,32,128]{2,1,0:T(8,128)(2,1)} %copy-done, f32[512,3]{1,0:T(8,128)} %copy.43.row_ref, f32[16,24,128]{2,1,0:T(8,128)} %copy-done.2), custom_call_target="tpu_custom_call" | custom-call | tf_op jit(solution)/shard_map/pallas_call | solution.py:183
  56.4 0.0 copy-start.3
  56.4 8.1 %all-to-all-start.2 = ((bf16[32,16,128]{2,1,0:T(8,128)(2,1)}), bf16[32,16,128]{2,1,0:T(8,128)(2,1)S(1)}, u32[]{:S(2)}, u32[]{:S(2)}) async-start(bf16[32,16,128]{2,1,0:T(8,128)(2,1)} %get-tuple-element.9), calls=%async_computation.2 | async-start | bytes 262144 | tf_op jit(solution)/shard_map/all_to_all | solution.py:232
  64.5 0.0 copy-done.3
  64.5 1.9 %all-gather.1 = bf16[128,512]{1,0:T(8,128)(2,1)S(1)} all-gather(bf16[64,512]{1,0:T(8,128)(2,1)S(1)} %copy-done.3), channel_id=3, replica_groups=mesh['xh'=2,'z3'=2,'z2'=2,'z1'=2,'z0'=2,'co'=2,'xl'=2,'y1'=2,'y0'=2] {'co'}, dimensions={0}, use_global_device_ids=true | all-gather | bytes 196608 | tf_op jit(solution)/shard_map/all_gather | solution.py:227
  66.4 7.8 %collective-permute-start.1 = (bf16[64,256]{1,0:T(8,128)(2,1)S(1)}, bf16[64,256]{1,0:T(8,128)(2,1)S(1)}, u32[]{:S(2)}, u32[]{:S(2)}) collective-permute-start(bf16[64,256]{1,0:T(8,128)(2,1)S(1)} %fusion), channel_id=1, source_target_pairs={{19,0},{83,1},{147,2},{211,3},{275,4},{339,5},{403,6},{467,7},{35,... | collective-permute-start | bytes 98312 | tf_op jit(solution)/shard_map/ppermute | solution.py:230
  74.3 6.3 %collective-permute-done.1 = bf16[64,256]{1,0:T(8,128)(2,1)S(1)} collective-permute-done((bf16[64,256]{1,0:T(8,128)(2,1)S(1)}, bf16[64,256]{1,0:T(8,128)(2,1)S(1)}, u32[]{:S(2)}, u32[]{:S(2)}) %collective-permute-start.1) | collective-permute-done | bytes 32800 | tf_op jit(solution)/shard_map/ppermute | solution.py:230
  80.5 3.2 %all_gather.27 = bf16[128,256]{1,0:T(8,128)(2,1)S(1)} all-gather(bf16[64,256]{1,0:T(8,128)(2,1)S(1)} %collective-permute-done.1), channel_id=1, replica_groups=mesh['xh'=2,'z3'=2,'z2'=2,'z1'=2,'z0'=2,'co'=2,'xl'=2,'y1'=2,'y0'=2] {'co'}, dimensions={0}, use_global_device_ids=true | all-gather | bytes 98304 | tf_op jit(solution)/shard_map/all_gather | solution.py:237
  83.7 0.7 copy.45
  84.4 0.0 all-to-all-done.2
  84.4 0.6 copy_bitcast_fusion
  (13 shorter events, 0.2 us)
Async XLA Ops:
  2.1 9.7 %copy-start.4 = (bf16[128,128]{1,0:T(8,128)(2,1)S(1)}, bf16[128,128]{1,0:T(8,128)(2,1)}, u32[]{:S(2)}) copy-start(bf16[128,128]{1,0:T(8,128)(2,1)} %param.4) | copy-start | bytes 98308
  2.1 34.3 %all-to-all-start = ((bf16[32,32,128]{2,1,0:T(8,128)(2,1)}), bf16[32,32,128]{2,1,0:T(8,128)(2,1)S(1)}, u32[]{:S(2)}, u32[]{:S(2)}) async-start(bf16[32,32,128]{2,1,0:T(8,128)(2,1)} %bitcast.3), calls=%async_computation | async-start | bytes 524288 | tf_op jit(solution)/shard_map/all_to_all | solution.py:220
  11.8 0.8 copy-start.5
  14.7 18.2 %collective-permute-start = (bf16[256,128]{0,1:T(8,128)(2,1)S(1)}, bf16[256,128]{0,1:T(8,128)(2,1)S(1)}, u32[]{:S(2)}, u32[]{:S(2)}) collective-permute-start(bf16[256,128]{0,1:T(8,128)(2,1)S(1)} %pad_maximum_fusion.1), channel_id=1, source_target_pairs={{0,19},{1,83},{2,147},{3,211},{4,275},{5,339},{6,403},{7,467},{8,3... | collective-permute-start | bytes 196616 | tf_op jit(solution)/shard_map/ppermute | solution.py:215
  35.7 0.8 copy-start.1
  36.4 0.7 copy-start
  40.7 6.1 %copy-start.6 = (f32[8,512]{1,0:T(8,128)S(1)}, f32[8,512]{1,0:T(8,128)}, u32[]{:S(2)}) copy-start(f32[8,512]{1,0:T(8,128)} %get-tuple-element.6) | copy-start | bytes 49156
  40.7 10.4 %all-to-all-start.1 = ((f32[16,24,128]{2,1,0:T(8,128)}), f32[16,24,128]{2,1,0:T(8,128)S(1)}, u32[]{:S(2)}, u32[]{:S(2)}) async-start(f32[16,24,128]{2,1,0:T(8,128)} %get-tuple-element.7), calls=%async_computation.1 | async-start | bytes 393216 | tf_op jit(solution)/shard_map/all_to_all | solution.py:223
  51.1 0.7 copy-start.2
  56.4 8.1 %copy-start.3 = (bf16[64,512]{1,0:T(8,128)(2,1)S(1)}, bf16[64,512]{1,0:T(8,128)(2,1)}, u32[]{:S(2)}) copy-start(bf16[64,512]{1,0:T(8,128)(2,1)} %get-tuple-element.8) | copy-start | bytes 196612
  56.4 28.1 %all-to-all-start.2 = ((bf16[32,16,128]{2,1,0:T(8,128)(2,1)}), bf16[32,16,128]{2,1,0:T(8,128)(2,1)S(1)}, u32[]{:S(2)}, u32[]{:S(2)}) async-start(bf16[32,16,128]{2,1,0:T(8,128)(2,1)} %get-tuple-element.9), calls=%async_computation.2 | async-start | bytes 262144 | tf_op jit(solution)/shard_map/all_to_all | solution.py:232
  66.4 14.1 %collective-permute-start.1 = (bf16[64,256]{1,0:T(8,128)(2,1)S(1)}, bf16[64,256]{1,0:T(8,128)(2,1)S(1)}, u32[]{:S(2)}, u32[]{:S(2)}) collective-permute-start(bf16[64,256]{1,0:T(8,128)(2,1)S(1)} %fusion), channel_id=1, source_target_pairs={{19,0},{83,1},{147,2},{211,3},{275,4},{339,5},{403,6},{467,7},{35,... | collective-permute-start | bytes 98312 | tf_op jit(solution)/shard_map/ppermute | solution.py:230

commit v5 on v4

--- a/solution.py
+++ b/solution.py
@@ -23,7 +23,7 @@
     for source in range(512):
         xh, z3, z2, z1, z0, co, xl, y1, y0 = ((source >> k) & 1 for k in range(8, -1, -1))
         target = 0
-        for bit in (xl, y1, y0, co, z0 ^ z1 ^ co ^ 1, z1, xh, 1 - z3, 1 - z2):
+        for bit in (xl, y1, y0, co, z0 ^ z1 ^ co ^ 1, z1, xh, 1 - z3, z2):
             target = 2 * target + bit
         pairs.append((source, target))
     return pairs
@@ -36,6 +36,7 @@
 BLOCK = 128
 CHUNK = 16
 LANES = 128
+LIMIT = 20 * 2**20
 
 
 def row_blocks(total, size):
@@ -95,7 +96,6 @@
 
 def slope_kernel(
     both,
-    turned,
     pieces,
     row_ref,
     column_ref,
@@ -132,6 +132,7 @@
 
     blocks = row_blocks(rows, BLOCK)
     products(blocks[0])
+    halves = []
     for n, block in enumerate(blocks):
         if n + 1 < len(blocks):
             products(blocks[n + 1])
@@ -152,9 +153,13 @@
                 r_ref[part, place] = row.astype(jnp.bfloat16)
                 c_ref[part, place] = column.astype(jnp.bfloat16)
         last = ((1,), (1,))
-        spec_out[:, block] = (
-            SCALE * dot(image[:SIZE, :], s_ref[block, :], last) + dot(image[SIZE:, :], c_ref[block, :], last)
-        ).astype(jnp.bfloat16)
+        part = SCALE * dot(s_ref[block, :], image[:SIZE, :], last)
+        part = part + dot(c_ref[block, :], image[SIZE:, :], last)
+        halves.append(part.astype(jnp.bfloat16))
+        if len(halves) == 2:
+            spec_out[n // 2] = jnp.concatenate(halves, axis=1)
+            halves = []
+    turned = both[...].astype(jnp.float32).T.astype(jnp.bfloat16)
     image_part = SCALE * dot(turned[:SIZE, :], s_ref[...], across) + dot(turned[SIZE:, :], r_ref[...], across)
     image_part = image_part.astype(jnp.bfloat16)
     size = SIZE // 4
@@ -172,25 +177,27 @@
             jax.ShapeDtypeStruct((peers, 3 * tokens // LANES, LANES), jnp.float32),
             jax.ShapeDtypeStruct((8, rows), jnp.float32),
         ),
+        compiler_params=pltpu.CompilerParams(vmem_limit_bytes=LIMIT),
         scratch_shapes=[wide, wide, wide, pltpu.VMEM((2 * SIZE, tokens), jnp.bfloat16)],
     )(both, image)
 
 
-def gradients(both, turned, image, row_stats, column_parts):
+def gradients(both, image, row_stats, column_parts):
     rows, tokens = both.shape[0], image.shape[0] // 4 * LANES
     wide = pltpu.VMEM((rows, tokens), jnp.float32)
     narrow = pltpu.VMEM((rows, tokens), jnp.bfloat16)
     return pl.pallas_call(
         slope_kernel,
         out_shape=(
-            jax.ShapeDtypeStruct((SIZE, rows), jnp.bfloat16),
+            jax.ShapeDtypeStruct((rows // (2 * BLOCK), BLOCK, 2 * SIZE), jnp.bfloat16),
             jax.ShapeDtypeStruct((4 * tokens // LANES, SIZE // 4, LANES), jnp.bfloat16),
         ),
+        compiler_params=pltpu.CompilerParams(vmem_limit_bytes=LIMIT),
         scratch_shapes=[
             *(wide, wide, wide, narrow, narrow, narrow),
             pltpu.VMEM((2 * SIZE, tokens), jnp.bfloat16),
         ],
-    )(both, turned, image, row_stats, column_parts)
+    )(both, image, row_stats, column_parts)
 
 
 def row_totals(parts):
@@ -205,7 +212,6 @@
     moves = head_moves()
     tokens = img_emb.shape[0]
     half = tokens // 2
-    rows = spec_emb.shape[0]
     second = lax.axis_index("co") == 1
     own = lax.all_gather(jnp.concatenate([spec_emb, grad_spec], axis=1), "co", tiled=True)
     own = jnp.concatenate(
@@ -223,9 +229,9 @@
     column_parts = lax.all_to_all(column_part, ROWS, 0, 0, tiled=True)
     row_parts = lax.all_gather(row_part, "co")
     row_stats = row_totals(row_parts)
-    spec_part, image_part = gradients(both, both.T, image, row_stats, column_parts)
+    spec_part, image_part = gradients(both, image, row_stats, column_parts)
     spec_parts = lax.all_gather(spec_part, "co")
-    spec_parts = jnp.where(second, spec_parts[:, :, 2 * rows :], spec_parts[:, :, : 2 * rows])
+    spec_parts = jnp.where(second, spec_parts[:, 1], spec_parts[:, 0])
     spec_sum = (spec_parts[0].astype(jnp.float32) + spec_parts[1]).astype(jnp.bfloat16)
     spec_back = lax.ppermute(spec_sum, EVERY, [(b, a) for a, b in moves])
 
@@ -234,8 +240,9 @@
     image_sum = jnp.sum(image_parts, axis=(0, 2)).astype(jnp.bfloat16)
     image_result = jnp.moveaxis(image_sum, 1, 2).reshape(tokens, SIZE // 4)
 
-    spec_heads = lax.all_gather(spec_back, "co", tiled=True)
-    spec_result = jnp.where(second, spec_heads[:, rows:], spec_heads[:, :rows]).T
+    spec_heads = lax.all_gather(spec_back, "co")
+    spec_heads = jnp.where(second, spec_heads[:, :, SIZE:], spec_heads[:, :, :SIZE])
+    spec_result = jnp.concatenate([spec_heads[0], spec_heads[1]], axis=1)
     return (spec_result, image_result)
 
 

time: 85.8 us -> 80.1 us (0.934)
  the two profiles are of different devices: /device:TPU:19 before, /device:TPU:1 now
where the time goes in v5:
time: 80.1 us; the launch traced here: 79.5 us
  starting transfers between devices  39.6 us (49%)
  waiting for transfers between devices  17.6 us (22%)
  blocking collectives  12.4 us (15%)
  Pallas kernels  5.8 us (7%)
  other arithmetic  1.83 us (2%)
  local copies, waits for them, and re-layouts  1.52 us (2%)
    all_to_all x1, starting transfers between devices, shards(): image = lax.all_to_all(image, GROUP, 0, 0, tiled=True)  10.5 us
    ppermute x1, starting transfers between devices, shards(): spec_back = lax.ppermute(spec_sum, EVERY, [(b, a) for a, b in moves])  10.5 us
    all_to_all x1, starting transfers between devices, shards(): column_parts = lax.all_to_all(column_part, ROWS, 0, 0, tiled=True)  9.07 us
    ppermute x1, waiting for transfers between devices, shards(): own = lax.ppermute(own, EVERY, moves)  8.27 us
    ppermute x1, starting transfers between devices, shards(): own = lax.ppermute(own, EVERY, moves)  5.74 us
    all_to_all x1, waiting for transfers between devices, shards(): column_parts = lax.all_to_all(column_part, ROWS, 0, 0, tiled=True)  4.67 us
    all_to_all x1, waiting for transfers between devices, shards(): image_parts = lax.all_to_all(image_part, GROUP, 0, 0, tiled=True)  4.65 us
    all_to_all x1, starting transfers between devices, shards(): image_parts = lax.all_to_all(image_part, GROUP, 0, 0, tiled=True)  3.7 us
  transfers between devices with their start and end apart: 5, of which 3 were waited for; matrix products, arithmetic and copies ran while one was open for 2% of the time, Pallas kernels for 0%

profile of v5, /device:TPU:1, one launch (start us, length us, event | category | flops | bytes accessed | tf_op | source)
XLA Modules:
  0.0 79.5 jit_solution(5324471498728667929)
XLA Ops:
  0.6 0.7 maximum_bitcast_fusion
  1.4 0.7 broadcast_in_dim.2
  2.1 0.0 copy-start
  2.1 0.0 copy-start.1
  2.1 10.5 %all-to-all-start = ((bf16[32,32,128]{2,1,0:T(8,128)(2,1)}), bf16[32,32,128]{2,1,0:T(8,128)(2,1)S(1)}, u32[]{:S(2)}, u32[]{:S(2)}) async-start(bf16[32,32,128]{2,1,0:T(8,128)(2,1)} %bitcast.2), calls=%async_computation | async-start | bytes 524288 | tf_op jit(solution)/shard_map/all_to_all | solution.py:226
  12.7 0.0 copy-done
  12.7 0.0 copy-done.1
  12.7 1.9 %all_gather.24 = bf16[256,256]{1,0:T(8,128)(2,1)S(1)} all-gather(bf16[128,256]{1,0:T(8,128)(2,1)S(1)} %pad_maximum_fusion), channel_id=1, replica_groups=mesh['xh'=2,'z3'=2,'z2'=2,'z1'=2,'z0'=2,'co'=2,'xl'=2,'y1'=2,'y0'=2] {'co'}, dimensions={0}, use_global_device_ids=true | all-gather | bytes 196608 | tf_op jit(solution)/shard_map/all_gather | solution.py:216
  14.6 0.1 slice_select_fusion.3
  14.7 0.1 pad_maximum_fusion.1
  14.8 5.7 %collective-permute-start = (bf16[256,128]{1,0:T(8,128)(2,1)S(1)}, bf16[256,128]{1,0:T(8,128)(2,1)S(1)}, u32[]{:S(2)}, u32[]{:S(2)}) collective-permute-start(bf16[256,128]{1,0:T(8,128)(2,1)S(1)} %pad_maximum_fusion.1), channel_id=1, source_target_pairs={{0,18},{1,82},{2,146},{3,210},{4,274},{5,338},{6,402},{7,466},{8,3... | collective-permute-start | bytes 196616 | tf_op jit(solution)/shard_map/ppermute | solution.py:221
  20.6 8.3 %collective-permute-done = bf16[256,128]{1,0:T(8,128)(2,1)S(1)} collective-permute-done((bf16[256,128]{1,0:T(8,128)(2,1)S(1)}, bf16[256,128]{1,0:T(8,128)(2,1)S(1)}, u32[]{:S(2)}, u32[]{:S(2)}) %collective-permute-start) | collective-permute-done | bytes 65568 | tf_op jit(solution)/shard_map/ppermute | solution.py:221
  28.8 3.3 %all_gather.25.both = bf16[512,128]{1,0:T(8,128)(2,1)S(1)} all-gather(bf16[256,128]{1,0:T(8,128)(2,1)S(1)} %collective-permute-done), channel_id=1, replica_groups=mesh['xh'=2,'z3'=2,'z2'=2,'z1'=2,'z0'=2,'co'=2,'xl'=2,'y1'=2,'y0'=2] {'co'}, dimensions={0}, use_global_device_ids=true | all-gather | bytes 196608 | tf_op jit(solution)/shard_map/all_gather | solution.py:227
  32.2 0.0 all-to-all-done.pieces
  32.2 2.4 %shard_map.59 = (f32[16,24,128]{2,1,0:T(8,128)}, f32[8,512]{1,0:T(8,128)S(1)}) custom-call(bf16[512,128]{1,0:T(8,128)(2,1)S(1)} %all_gather.25.both, bf16[32,32,128]{2,1,0:T(8,128)(2,1)S(1)} %all-to-all-done.pieces), custom_call_target="tpu_custom_call" | custom-call | tf_op jit(solution)/shard_map/pallas_call | solution.py:174
  34.6 9.1 %all-to-all-start.1 = ((f32[16,24,128]{2,1,0:T(8,128)}), f32[16,24,128]{2,1,0:T(8,128)S(1)}, u32[]{:S(2)}, u32[]{:S(2)}) async-start(f32[16,24,128]{2,1,0:T(8,128)} %get-tuple-element.7), calls=%async_computation.1 | async-start | bytes 393216 | tf_op jit(solution)/shard_map/all_to_all | solution.py:229
  43.6 2.1 %all-gather = f32[16,512]{1,0:T(8,128)S(1)} all-gather(f32[8,512]{1,0:T(8,128)S(1)} %get-tuple-element.6), channel_id=2, replica_groups=mesh['xh'=2,'z3'=2,'z2'=2,'z1'=2,'z0'=2,'co'=2,'xl'=2,'y1'=2,'y0'=2] {'co'}, dimensions={0}, use_global_device_ids=true | all-gather | bytes 49152 | tf_op jit(solution)/shard_map/all_gather | solution.py:230
  45.8 0.1 copy.22.row_ref
  46.0 4.7 %all-to-all-done.1.column_ref = f32[16,24,128]{2,1,0:T(8,128)S(1)} async-done(((f32[16,24,128]{2,1,0:T(8,128)}), f32[16,24,128]{2,1,0:T(8,128)S(1)}, u32[]{:S(2)}, u32[]{:S(2)}) %all-to-all-start.1) | async-done | bytes 196640 | tf_op jit(solution)/shard_map/all_to_all | solution.py:229
  50.7 3.4 %shard_map.60 = (bf16[2,128,128]{2,1,0:T(8,128)(2,1)S(1)}, bf16[32,16,128]{2,1,0:T(8,128)(2,1)}) custom-call(bf16[512,128]{1,0:T(8,128)(2,1)S(1)} %all_gather.25.both, bf16[32,32,128]{2,1,0:T(8,128)(2,1)S(1)} %all-to-all-done.pieces, f32[512,3]{1,0:T(8,128)S(1)} %copy.22.row_ref, f32[16,24,128]{2,1,0:T(8,128)S(1)} %all-to-all-done.1.column_ref), custom_call_target="tpu_custom_call" | custom-call | tf_op jit(solution)/shard_map/pallas_call | solution.py:189
  54.1 3.2 %all-gather.1 = bf16[4,128,128]{2,1,0:T(8,128)(2,1)S(1)} all-gather(bf16[2,128,128]{2,1,0:T(8,128)(2,1)S(1)} %get-tuple-element.8), channel_id=3, replica_groups=mesh['xh'=2,'z3'=2,'z2'=2,'z1'=2,'z0'=2,'co'=2,'xl'=2,'y1'=2,'y0'=2] {'co'}, dimensions={0}, use_global_device_ids=true | all-gather | bytes 196608 | tf_op jit(solution)/shard_map/all_gather | solution.py:233
  57.3 10.5 %collective-permute-start.1 = (bf16[128,128]{1,0:T(8,128)(2,1)S(1)}, bf16[128,128]{1,0:T(8,128)(2,1)S(1)}, u32[]{:S(2)}, u32[]{:S(2)}) collective-permute-start(bf16[128,128]{1,0:T(8,128)(2,1)S(1)} %fusion), channel_id=1, source_target_pairs={{18,0},{82,1},{146,2},{210,3},{274,4},{338,5},{402,6},{466,7},{34,... | collective-permute-start | bytes 98312 | tf_op jit(solution)/shard_map/ppermute | solution.py:236
  67.8 3.7 %all-to-all-start.2 = ((bf16[32,16,128]{2,1,0:T(8,128)(2,1)}), bf16[32,16,128]{2,1,0:T(8,128)(2,1)S(1)}, u32[]{:S(2)}, u32[]{:S(2)}) async-start(bf16[32,16,128]{2,1,0:T(8,128)(2,1)} %get-tuple-element.9), calls=%async_computation.2 | async-start | bytes 262144 | tf_op jit(solution)/shard_map/all_to_all | solution.py:238
  71.5 0.0 collective-permute-done.1
  71.6 1.9 %all-gather.2 = bf16[256,128]{1,0:T(8,128)(2,1)S(1)} all-gather(bf16[128,128]{1,0:T(8,128)(2,1)S(1)} %collective-permute-done.1), channel_id=4, replica_groups=mesh['xh'=2,'z3'=2,'z2'=2,'z1'=2,'z0'=2,'co'=2,'xl'=2,'y1'=2,'y0'=2] {'co'}, dimensions={0}, use_global_device_ids=true | all-gather | bytes 98304 | tf_op jit(solution)/shard_map/all_gather | solution.py:243
  73.4 0.1 slice_select_fusion
  73.5 0.7 pad_maximum_fusion.2
  74.2 4.7 %all-to-all-done.2 = bf16[32,16,128]{2,1,0:T(8,128)(2,1)S(1)} async-done(((bf16[32,16,128]{2,1,0:T(8,128)(2,1)}), bf16[32,16,128]{2,1,0:T(8,128)(2,1)S(1)}, u32[]{:S(2)}, u32[]{:S(2)}) %all-to-all-start.2) | async-done | bytes 131104 | tf_op jit(solution)/shard_map/all_to_all | solution.py:238
  78.9 0.6 copy_bitcast_fusion
  (11 shorter events, 0.2 us)
Async XLA Ops:
  2.1 10.6 %copy-start = (bf16[128,128]{1,0:T(8,128)(2,1)S(1)}, bf16[128,128]{1,0:T(8,128)(2,1)}, u32[]{:S(2)}) copy-start(bf16[128,128]{1,0:T(8,128)(2,1)} %param.6) | copy-start | bytes 98308
  2.1 10.6 %copy-start.1 = (bf16[128,128]{1,0:T(8,128)(2,1)S(1)}, bf16[128,128]{1,0:T(8,128)(2,1)}, u32[]{:S(2)}) copy-start(bf16[128,128]{1,0:T(8,128)(2,1)} %param.4) | copy-start | bytes 98308
  2.1 30.1 %all-to-all-start = ((bf16[32,32,128]{2,1,0:T(8,128)(2,1)}), bf16[32,32,128]{2,1,0:T(8,128)(2,1)S(1)}, u32[]{:S(2)}, u32[]{:S(2)}) async-start(bf16[32,32,128]{2,1,0:T(8,128)(2,1)} %bitcast.2), calls=%async_computation | async-start | bytes 524288 | tf_op jit(solution)/shard_map/all_to_all | solution.py:226
  14.8 14.0 %collective-permute-start = (bf16[256,128]{1,0:T(8,128)(2,1)S(1)}, bf16[256,128]{1,0:T(8,128)(2,1)S(1)}, u32[]{:S(2)}, u32[]{:S(2)}) collective-permute-start(bf16[256,128]{1,0:T(8,128)(2,1)S(1)} %pad_maximum_fusion.1), channel_id=1, source_target_pairs={{0,18},{1,82},{2,146},{3,210},{4,274},{5,338},{6,402},{7,466},{8,3... | collective-permute-start | bytes 196616 | tf_op jit(solution)/shard_map/ppermute | solution.py:221
  34.6 16.1 %all-to-all-start.1 = ((f32[16,24,128]{2,1,0:T(8,128)}), f32[16,24,128]{2,1,0:T(8,128)S(1)}, u32[]{:S(2)}, u32[]{:S(2)}) async-start(f32[16,24,128]{2,1,0:T(8,128)} %get-tuple-element.7), calls=%async_computation.1 | async-start | bytes 393216 | tf_op jit(solution)/shard_map/all_to_all | solution.py:229
  57.3 14.2 %collective-permute-start.1 = (bf16[128,128]{1,0:T(8,128)(2,1)S(1)}, bf16[128,128]{1,0:T(8,128)(2,1)S(1)}, u32[]{:S(2)}, u32[]{:S(2)}) collective-permute-start(bf16[128,128]{1,0:T(8,128)(2,1)S(1)} %fusion), channel_id=1, source_target_pairs={{18,0},{82,1},{146,2},{210,3},{274,4},{338,5},{402,6},{466,7},{34,... | collective-permute-start | bytes 98312 | tf_op jit(solution)/shard_map/ppermute | solution.py:236
  67.8 11.0 %all-to-all-start.2 = ((bf16[32,16,128]{2,1,0:T(8,128)(2,1)}), bf16[32,16,128]{2,1,0:T(8,128)(2,1)S(1)}, u32[]{:S(2)}, u32[]{:S(2)}) async-start(bf16[32,16,128]{2,1,0:T(8,128)(2,1)} %get-tuple-element.9), calls=%async_computation.2 | async-start | bytes 262144 | tf_op jit(solution)/shard_map/all_to_all | solution.py:238

commit v6 on v5

--- a/solution.py
+++ b/solution.py
@@ -54,7 +54,7 @@
                 )
 
 
-def stats_kernel(both, pieces, column_out, row_out, z_ref, p_ref, q_ref, image):
+def stats_kernel(both, pieces, column_out, row_out, z_ref, p_ref, q_ref, image, piece_ref, sems):
     rows, tokens = z_ref.shape
     unpack(pieces, image)
     peak = None
@@ -62,57 +62,71 @@
         z = dot(both[block, :SIZE], image[:SIZE, :], ((1,), (0,))) * SCALE
         z_ref[block, :] = z
         q_ref[block, :] = dot(both[block, :SIZE], image[SIZE:, :], ((1,), (0,)))
-        p_ref[block, :] = dot(both[block, SIZE:], image[:SIZE, :], ((1,), (0,)))
         for part in row_blocks(BLOCK, 8):
             peak = z[part] if peak is None else jnp.maximum(peak, z[part])
     high = jnp.max(peak, axis=0, keepdims=True)
     total = jnp.zeros((8, tokens), jnp.float32)
     weighted = jnp.zeros((8, tokens), jnp.float32)
-    lane = lax.broadcasted_iota(jnp.int32, (8, LANES), 1)
-    columns = []
     for part in row_blocks(rows, 8):
-        z = z_ref[part, :]
-        scaled = jnp.exp(z - high)
+        scaled = jnp.exp(z_ref[part, :] - high)
         total = total + scaled
         weighted = weighted + scaled * q_ref[part, :]
-        row_high = jnp.max(z, axis=1, keepdims=True)
-        scaled = jnp.exp(z - row_high)
-        row_total = jnp.sum(scaled, axis=1, keepdims=True)
-        row_weighted = jnp.sum(scaled * p_ref[part, :], axis=1, keepdims=True)
-        columns.append(jnp.where(lane == 0, row_high, jnp.where(lane == 1, row_total, row_weighted)))
-        if len(columns) * 8 == LANES:
-            base = part.stop - LANES
-            row_out[:, base : base + LANES] = jnp.concatenate(columns, axis=0).T[:8]
-            columns = []
     sums = (
         high,
         jnp.sum(total, axis=0, keepdims=True),
         jnp.sum(weighted, axis=0, keepdims=True),
     )
-    piece = jnp.concatenate([v[:, k] for v in sums for k in row_blocks(tokens, LANES)], axis=0)
-    for peer in range(column_out.shape[0]):
-        column_out[peer] = piece
+    piece_ref[...] = jnp.concatenate([v[:, k] for v in sums for k in row_blocks(tokens, LANES)], axis=0)
+    copies = [
+        pltpu.make_async_copy(piece_ref, column_out.at[peer], sems.at[peer])
+        for peer in range(column_out.shape[0])
+    ]
+    for copy in copies:
+        copy.start()
+    lane = lax.broadcasted_iota(jnp.int32, (8, LANES), 1)
+    for block in row_blocks(rows, BLOCK):
+        p_ref[block, :] = dot(both[block, SIZE:], image[:SIZE, :], ((1,), (0,)))
+    for block in row_blocks(rows, LANES):
+        columns = []
+        for start in range(block.start, block.stop, 8):
+            part = slice(start, start + 8)
+            z = z_ref[part, :]
+            row_high = jnp.max(z, axis=1, keepdims=True)
+            scaled = jnp.exp(z - row_high)
+            row_total = jnp.sum(scaled, axis=1, keepdims=True)
+            row_weighted = jnp.sum(scaled * p_ref[part, :], axis=1, keepdims=True)
+            columns.append(
+                jnp.where(lane == 0, row_high, jnp.where(lane == 1, row_total, row_weighted))
+            )
+        row_out[:, block] = jnp.concatenate(columns, axis=0).T[:8]
+    for copy in copies:
+        copy.wait()
+
+
+def row_kernel(both, pieces, row_ref, slope_out, image_out, z_ref, p_ref, r_ref, image):
+    rows, tokens = z_ref.shape
+    unpack(pieces, image)
+    for block in row_blocks(rows, BLOCK):
+        z_ref[block, :] = dot(both[block, :SIZE], image[:SIZE, :], ((1,), (0,))) * SCALE
+        p_ref[block, :] = dot(both[block, SIZE:], image[:SIZE, :], ((1,), (0,)))
+    for part in row_blocks(rows, CHUNK):
+        row_high = jnp.broadcast_to(row_ref[part, 0:1], (CHUNK, LANES))
+        row_shrink = jnp.broadcast_to(row_ref[part, 1:2], (CHUNK, LANES))
+        row_delta = jnp.broadcast_to(row_ref[part, 2:3], (CHUNK, LANES))
+        for place in row_blocks(tokens, LANES):
+            row = jnp.exp(z_ref[part, place] - row_high) * row_shrink
+            slope_out[part, place] = row * (p_ref[part, place] - row_delta)
+            r_ref[part, place] = row.astype(jnp.bfloat16)
+    turned = both[:, SIZE:].astype(jnp.float32).T.astype(jnp.bfloat16)
+    image_out[...] = dot(turned, r_ref[...], ((1,), (0,)))
 
 
 def slope_kernel(
-    both,
-    pieces,
-    row_ref,
-    column_ref,
-    spec_out,
-    image_out,
-    z_ref,
-    p_ref,
-    q_ref,
-    s_ref,
-    r_ref,
-    c_ref,
-    image,
+    both, pieces, column_ref, row_slope, row_image, spec_out, image_out, z_ref, q_ref, s_ref, c_ref, image
 ):
     rows, tokens = z_ref.shape
     unpack(pieces, image)
     groups = tokens // LANES
-    across = ((1,), (0,))
     peers = column_ref.shape[0]
     high = column_ref[0, :groups]
     for peer in range(1, peers):
@@ -124,11 +138,12 @@
         weighted = weighted + column_ref[peer, 2 * groups :] * factor
     shrink = 1.0 / total
     delta = weighted * shrink
+    turned = both[:, :SIZE].astype(jnp.float32).T.astype(jnp.bfloat16)
+    image_part = row_image[...]
 
     def products(block):
-        z_ref[block, :] = dot(both[block, :SIZE], image[:SIZE, :], across) * SCALE
-        p_ref[block, :] = dot(both[block, SIZE:], image[:SIZE, :], across)
-        q_ref[block, :] = dot(both[block, :SIZE], image[SIZE:, :], across)
+        z_ref[block, :] = dot(both[block, :SIZE], image[:SIZE, :], ((1,), (0,))) * SCALE
+        q_ref[block, :] = dot(both[block, :SIZE], image[SIZE:, :], ((1,), (0,)))
 
     blocks = row_blocks(rows, BLOCK)
     products(blocks[0])
@@ -138,19 +153,11 @@
             products(blocks[n + 1])
         for part in row_blocks(BLOCK, CHUNK):
             part = slice(block.start + part.start, block.start + part.stop)
-            row_high = jnp.broadcast_to(row_ref[part, 0:1], (CHUNK, LANES))
-            row_shrink = jnp.broadcast_to(row_ref[part, 1:2], (CHUNK, LANES))
-            row_delta = jnp.broadcast_to(row_ref[part, 2:3], (CHUNK, LANES))
             for k in range(groups):
                 place = slice(k * LANES, (k + 1) * LANES)
-                z = z_ref[part, place]
-                row = jnp.exp(z - row_high) * row_shrink
-                column = jnp.exp(z - high[k : k + 1]) * shrink[k : k + 1]
-                slope = row * (p_ref[part, place] - row_delta) + column * (
-                    q_ref[part, place] - delta[k : k + 1]
-                )
+                column = jnp.exp(z_ref[part, place] - high[k : k + 1]) * shrink[k : k + 1]
+                slope = row_slope[part, place] + column * (q_ref[part, place] - delta[k : k + 1])
                 s_ref[part, place] = slope.astype(jnp.bfloat16)
-                r_ref[part, place] = row.astype(jnp.bfloat16)
                 c_ref[part, place] = column.astype(jnp.bfloat16)
         last = ((1,), (1,))
         part = SCALE * dot(s_ref[block, :], image[:SIZE, :], last)
@@ -159,8 +166,7 @@
         if len(halves) == 2:
             spec_out[n // 2] = jnp.concatenate(halves, axis=1)
             halves = []
-    turned = both[...].astype(jnp.float32).T.astype(jnp.bfloat16)
-    image_part = SCALE * dot(turned[:SIZE, :], s_ref[...], across) + dot(turned[SIZE:, :], r_ref[...], across)
+    image_part = image_part + SCALE * dot(turned, s_ref[...], ((1,), (0,)))
     image_part = image_part.astype(jnp.bfloat16)
     size = SIZE // 4
     for f in range(4):
@@ -168,22 +174,48 @@
             image_out[f * groups + k] = image_part[f * size : (f + 1) * size, k * LANES : (k + 1) * LANES]
 
 
-def statistics(both, image, peers):
-    rows, tokens = both.shape[0], image.shape[0] // 4 * LANES
+def statistics(both, pieces, peers):
+    rows, tokens = both.shape[0], pieces.shape[0] // 4 * LANES
     wide = pltpu.VMEM((rows, tokens), jnp.float32)
+    whole = pl.BlockSpec(memory_space=pltpu.VMEM)
     return pl.pallas_call(
         stats_kernel,
         out_shape=(
             jax.ShapeDtypeStruct((peers, 3 * tokens // LANES, LANES), jnp.float32),
             jax.ShapeDtypeStruct((8, rows), jnp.float32),
         ),
+        in_specs=(whole, whole),
+        out_specs=(pl.BlockSpec(memory_space=pl.ANY), whole),
         compiler_params=pltpu.CompilerParams(vmem_limit_bytes=LIMIT),
-        scratch_shapes=[wide, wide, wide, pltpu.VMEM((2 * SIZE, tokens), jnp.bfloat16)],
-    )(both, image)
-
-
-def gradients(both, image, row_stats, column_parts):
-    rows, tokens = both.shape[0], image.shape[0] // 4 * LANES
+        scratch_shapes=[
+            *(wide, wide, wide),
+            pltpu.VMEM((2 * SIZE, tokens), jnp.bfloat16),
+            pltpu.VMEM((3 * tokens // LANES, LANES), jnp.float32),
+            pltpu.SemaphoreType.DMA((peers,)),
+        ],
+    )(both, pieces)
+
+
+def row_side(both, pieces, row_stats):
+    rows, tokens = both.shape[0], pieces.shape[0] // 4 * LANES
+    wide = pltpu.VMEM((rows, tokens), jnp.float32)
+    return pl.pallas_call(
+        row_kernel,
+        out_shape=(
+            jax.ShapeDtypeStruct((rows, tokens), jnp.float32),
+            jax.ShapeDtypeStruct((SIZE, tokens), jnp.float32),
+        ),
+        compiler_params=pltpu.CompilerParams(vmem_limit_bytes=LIMIT),
+        scratch_shapes=[
+            *(wide, wide),
+            pltpu.VMEM((rows, tokens), jnp.bfloat16),
+            pltpu.VMEM((2 * SIZE, tokens), jnp.bfloat16),
+        ],
+    )(both, pieces, row_stats)
+
+
+def gradients(both, pieces, column_parts, row_slope, row_image):
+    rows, tokens = row_slope.shape
     wide = pltpu.VMEM((rows, tokens), jnp.float32)
     narrow = pltpu.VMEM((rows, tokens), jnp.bfloat16)
     return pl.pallas_call(
@@ -194,10 +226,10 @@
         ),
         compiler_params=pltpu.CompilerParams(vmem_limit_bytes=LIMIT),
         scratch_shapes=[
-            *(wide, wide, wide, narrow, narrow, narrow),
+            *(wide, wide, narrow, narrow),
             pltpu.VMEM((2 * SIZE, tokens), jnp.bfloat16),
         ],
-    )(both, image, row_stats, column_parts)
+    )(both, pieces, column_parts, row_slope, row_image)
 
 
 def row_totals(parts):
@@ -229,7 +261,8 @@
     column_parts = lax.all_to_all(column_part, ROWS, 0, 0, tiled=True)
     row_parts = lax.all_gather(row_part, "co")
     row_stats = row_totals(row_parts)
-    spec_part, image_part = gradients(both, image, row_stats, column_parts)
+    row_slope, row_image = row_side(both, image, row_stats)
+    spec_part, image_part = gradients(both, image, column_parts, row_slope, row_image)
     spec_parts = lax.all_gather(spec_part, "co")
     spec_parts = jnp.where(second, spec_parts[:, 1], spec_parts[:, 0])
     spec_sum = (spec_parts[0].astype(jnp.float32) + spec_parts[1]).astype(jnp.bfloat16)

time: 80.1 us -> 79.7 us (level)
  waiting for transfers between devices: 17.6 us -> 16.4 us
    all_to_all x1, waiting for transfers between devices: 4.67 us -> 3.46 us  [shards(): column_parts = lax.all_to_all(column_part, ROWS, 0, 0, tiled=True)]
    pallas_call x0 -> x1, Pallas kernels: none -> 1.2 us  [row_side(): pl.pallas_call(row_kernel, out_shape=(jax.ShapeDtypeStruct((rows, tokens)...]
    pallas_call x1, Pallas kernels: 3.43 us -> 2.37 us  [gradients(): pl.pallas_call(slope_kernel, out_shape=(jax.ShapeDtypeStruct((rows // (2...]
  transfers between devices with their start and end apart: 5 -> 5, of which waited for: 3 -> 3; matrix products, arithmetic and copies ran while one was open for 2% -> 3% of each run, Pallas kernels for 0% -> 2%
where the time goes in v6:
time: 79.7 us; the launch traced here: 79.1 us
  starting transfers between devices  39.5 us (50%)
  waiting for transfers between devices  16.4 us (21%)
  blocking collectives  12.4 us (16%)
  Pallas kernels  5.93 us (7%)
  other arithmetic  2.61 us (3%)
  local copies, waits for them, and re-layouts  1.51 us (2%)
    ppermute x1, starting transfers between devices, shards(): spec_back = lax.ppermute(spec_sum, EVERY, [(b, a) for a, b in moves])  10.5 us
    all_to_all x1, starting transfers between devices, shards(): image = lax.all_to_all(image, GROUP, 0, 0, tiled=True)  10.4 us
    all_to_all x1, starting transfers between devices, shards(): column_parts = lax.all_to_all(column_part, ROWS, 0, 0, tiled=True)  9.08 us
    ppermute x1, waiting for transfers between devices, shards(): own = lax.ppermute(own, EVERY, moves)  8.27 us
    ppermute x1, starting transfers between devices, shards(): own = lax.ppermute(own, EVERY, moves)  5.74 us
    all_to_all x1, waiting for transfers between devices, shards(): image_parts = lax.all_to_all(image_part, GROUP, 0, 0, tiled=True)  4.65 us
    all_to_all x1, starting transfers between devices, shards(): image_parts = lax.all_to_all(image_part, GROUP, 0, 0, tiled=True)  3.69 us
    all_to_all x1, waiting for transfers between devices, shards(): column_parts = lax.all_to_all(column_part, ROWS, 0, 0, tiled=True)  3.46 us
  transfers between devices with their start and end apart: 5, of which 3 were waited for; matrix products, arithmetic and copies ran while one was open for 3% of the time, Pallas kernels for 2%

profile of v6, /device:TPU:1, one launch (start us, length us, event | category | flops | bytes accessed | tf_op | source)
XLA Modules:
  0.0 79.1 jit_solution(17541583948545877834)
XLA Ops:
  0.6 0.7 maximum_bitcast_fusion
  1.4 0.7 broadcast_in_dim.2
  2.1 10.4 %all-to-all-start = ((bf16[32,32,128]{2,1,0:T(8,128)(2,1)}), bf16[32,32,128]{2,1,0:T(8,128)(2,1)S(1)}, u32[]{:S(2)}, u32[]{:S(2)}) async-start(bf16[32,32,128]{2,1,0:T(8,128)(2,1)} %bitcast.2), calls=%async_computation | async-start | bytes 524288 | tf_op jit(solution)/shard_map/all_to_all | solution.py:258
  12.5 0.8 pad_maximum_fusion
  13.3 1.9 %all_gather.24 = bf16[256,256]{1,0:T(8,128)(2,1)S(1)} all-gather(bf16[128,256]{1,0:T(8,128)(2,1)S(1)} %pad_maximum_fusion), channel_id=1, replica_groups=mesh['xh'=2,'z3'=2,'z2'=2,'z1'=2,'z0'=2,'co'=2,'xl'=2,'y1'=2,'y0'=2] {'co'}, dimensions={0}, use_global_device_ids=true | all-gather | bytes 196608 | tf_op jit(solution)/shard_map/all_gather | solution.py:248
  15.2 0.1 slice_select_fusion.3
  15.3 0.1 pad_maximum_fusion.1
  15.4 5.7 %collective-permute-start = (bf16[256,128]{1,0:T(8,128)(2,1)S(1)}, bf16[256,128]{1,0:T(8,128)(2,1)S(1)}, u32[]{:S(2)}, u32[]{:S(2)}) collective-permute-start(bf16[256,128]{1,0:T(8,128)(2,1)S(1)} %pad_maximum_fusion.1), channel_id=1, source_target_pairs={{0,18},{1,82},{2,146},{3,210},{4,274},{5,338},{6,402},{7,466},{8,3... | collective-permute-start | bytes 196616 | tf_op jit(solution)/shard_map/ppermute | solution.py:253
  21.2 8.3 %collective-permute-done = bf16[256,128]{1,0:T(8,128)(2,1)S(1)} collective-permute-done((bf16[256,128]{1,0:T(8,128)(2,1)S(1)}, bf16[256,128]{1,0:T(8,128)(2,1)S(1)}, u32[]{:S(2)}, u32[]{:S(2)}) %collective-permute-start) | collective-permute-done | bytes 65568 | tf_op jit(solution)/shard_map/ppermute | solution.py:253
  29.4 3.3 %all_gather.25.both = bf16[512,128]{1,0:T(8,128)(2,1)S(1)} all-gather(bf16[256,128]{1,0:T(8,128)(2,1)S(1)} %collective-permute-done), channel_id=1, replica_groups=mesh['xh'=2,'z3'=2,'z2'=2,'z1'=2,'z0'=2,'co'=2,'xl'=2,'y1'=2,'y0'=2] {'co'}, dimensions={0}, use_global_device_ids=true | all-gather | bytes 196608 | tf_op jit(solution)/shard_map/all_gather | solution.py:259
  32.8 0.0 all-to-all-done.pieces
  32.8 2.4 %shard_map.59 = (f32[16,24,128]{2,1,0:T(8,128)}, f32[8,512]{1,0:T(8,128)S(1)}) custom-call(bf16[512,128]{1,0:T(8,128)(2,1)S(1)} %all_gather.25.both, bf16[32,32,128]{2,1,0:T(8,128)(2,1)S(1)} %all-to-all-done.pieces), custom_call_target="tpu_custom_call" | custom-call | tf_op jit(solution)/shard_map/pallas_call | solution.py:181
  35.2 9.1 %all-to-all-start.1 = ((f32[16,24,128]{2,1,0:T(8,128)}), f32[16,24,128]{2,1,0:T(8,128)S(1)}, u32[]{:S(2)}, u32[]{:S(2)}) async-start(f32[16,24,128]{2,1,0:T(8,128)} %get-tuple-element.8), calls=%async_computation.1 | async-start | bytes 393216 | tf_op jit(solution)/shard_map/all_to_all | solution.py:261
  44.2 2.1 %all-gather = f32[16,512]{1,0:T(8,128)S(1)} all-gather(f32[8,512]{1,0:T(8,128)S(1)} %get-tuple-element.9), channel_id=2, replica_groups=mesh['xh'=2,'z3'=2,'z2'=2,'z1'=2,'z0'=2,'co'=2,'xl'=2,'y1'=2,'y0'=2] {'co'}, dimensions={0}, use_global_device_ids=true | all-gather | bytes 49152 | tf_op jit(solution)/shard_map/all_gather | solution.py:262
  46.4 0.1 copy.22.row_ref
  46.6 1.2 %shard_map.60 = (f32[512,1024]{1,0:T(8,128)S(1)}, f32[64,1024]{1,0:T(8,128)S(1)}) custom-call(bf16[512,128]{1,0:T(8,128)(2,1)S(1)} %all_gather.25.both, bf16[32,32,128]{2,1,0:T(8,128)(2,1)S(1)} %all-to-all-done.pieces, f32[512,3]{1,0:T(8,128)S(1)} %copy.22.row_ref), custom_call_target="tpu_custom_call" | custom-call | tf_op jit(solution)/shard_map/pallas_call | solution.py:202
  47.8 3.5 %all-to-all-done.1.column_ref = f32[16,24,128]{2,1,0:T(8,128)S(1)} async-done(((f32[16,24,128]{2,1,0:T(8,128)}), f32[16,24,128]{2,1,0:T(8,128)S(1)}, u32[]{:S(2)}, u32[]{:S(2)}) %all-to-all-start.1) | async-done | bytes 196640 | tf_op jit(solution)/shard_map/all_to_all | solution.py:261
  51.3 2.4 %shard_map.61 = (bf16[2,128,128]{2,1,0:T(8,128)(2,1)S(1)}, bf16[32,16,128]{2,1,0:T(8,128)(2,1)}) custom-call(bf16[512,128]{1,0:T(8,128)(2,1)S(1)} %all_gather.25.both, bf16[32,32,128]{2,1,0:T(8,128)(2,1)S(1)} %all-to-all-done.pieces, f32[16,24,128]{2,1,0:T(8,128)S(1)} %all-to-all-done.1.column_ref, f32[512,1024]{1,0:T(8,128)S(1)} %get-tuple-element.10.row_slope, ...), custom_call_target="tpu_custom_call" | custom-call | tf_op jit(solution)/shard_map/pallas_call | solution.py:221
  53.6 3.2 %all-gather.1 = bf16[4,128,128]{2,1,0:T(8,128)(2,1)S(1)} all-gather(bf16[2,128,128]{2,1,0:T(8,128)(2,1)S(1)} %get-tuple-element.12), channel_id=3, replica_groups=mesh['xh'=2,'z3'=2,'z2'=2,'z1'=2,'z0'=2,'co'=2,'xl'=2,'y1'=2,'y0'=2] {'co'}, dimensions={0}, use_global_device_ids=true | all-gather | bytes 196608 | tf_op jit(solution)/shard_map/all_gather | solution.py:266
  56.9 10.5 %collective-permute-start.1 = (bf16[128,128]{1,0:T(8,128)(2,1)S(1)}, bf16[128,128]{1,0:T(8,128)(2,1)S(1)}, u32[]{:S(2)}, u32[]{:S(2)}) collective-permute-start(bf16[128,128]{1,0:T(8,128)(2,1)S(1)} %fusion), channel_id=1, source_target_pairs={{18,0},{82,1},{146,2},{210,3},{274,4},{338,5},{402,6},{466,7},{34,... | collective-permute-start | bytes 98312 | tf_op jit(solution)/shard_map/ppermute | solution.py:269
  67.4 3.7 %all-to-all-start.2 = ((bf16[32,16,128]{2,1,0:T(8,128)(2,1)}), bf16[32,16,128]{2,1,0:T(8,128)(2,1)S(1)}, u32[]{:S(2)}, u32[]{:S(2)}) async-start(bf16[32,16,128]{2,1,0:T(8,128)(2,1)} %get-tuple-element.13), calls=%async_computation.2 | async-start | bytes 262144 | tf_op jit(solution)/shard_map/all_to_all | solution.py:271
  71.1 0.0 collective-permute-done.1
  71.1 1.9 %all-gather.2 = bf16[256,128]{1,0:T(8,128)(2,1)S(1)} all-gather(bf16[128,128]{1,0:T(8,128)(2,1)S(1)} %collective-permute-done.1), channel_id=4, replica_groups=mesh['xh'=2,'z3'=2,'z2'=2,'z1'=2,'z0'=2,'co'=2,'xl'=2,'y1'=2,'y0'=2] {'co'}, dimensions={0}, use_global_device_ids=true | all-gather | bytes 98304 | tf_op jit(solution)/shard_map/all_gather | solution.py:276
  73.0 0.1 slice_select_fusion
  73.1 0.7 pad_maximum_fusion.2
  73.8 4.7 %all-to-all-done.2 = bf16[32,16,128]{2,1,0:T(8,128)(2,1)S(1)} async-done(((bf16[32,16,128]{2,1,0:T(8,128)(2,1)}), bf16[32,16,128]{2,1,0:T(8,128)(2,1)S(1)}, u32[]{:S(2)}, u32[]{:S(2)}) %all-to-all-start.2) | async-done | bytes 131104 | tf_op jit(solution)/shard_map/all_to_all | solution.py:271
  78.5 0.6 copy_bitcast_fusion
  (10 shorter events, 0.1 us)
Async XLA Ops:
  2.1 30.7 %all-to-all-start = ((bf16[32,32,128]{2,1,0:T(8,128)(2,1)}), bf16[32,32,128]{2,1,0:T(8,128)(2,1)S(1)}, u32[]{:S(2)}, u32[]{:S(2)}) async-start(bf16[32,32,128]{2,1,0:T(8,128)(2,1)} %bitcast.2), calls=%async_computation | async-start | bytes 524288 | tf_op jit(solution)/shard_map/all_to_all | solution.py:258
  15.4 14.0 %collective-permute-start = (bf16[256,128]{1,0:T(8,128)(2,1)S(1)}, bf16[256,128]{1,0:T(8,128)(2,1)S(1)}, u32[]{:S(2)}, u32[]{:S(2)}) collective-permute-start(bf16[256,128]{1,0:T(8,128)(2,1)S(1)} %pad_maximum_fusion.1), channel_id=1, source_target_pairs={{0,18},{1,82},{2,146},{3,210},{4,274},{5,338},{6,402},{7,466},{8,3... | collective-permute-start | bytes 196616 | tf_op jit(solution)/shard_map/ppermute | solution.py:253
  35.2 16.1 %all-to-all-start.1 = ((f32[16,24,128]{2,1,0:T(8,128)}), f32[16,24,128]{2,1,0:T(8,128)S(1)}, u32[]{:S(2)}, u32[]{:S(2)}) async-start(f32[16,24,128]{2,1,0:T(8,128)} %get-tuple-element.8), calls=%async_computation.1 | async-start | bytes 393216 | tf_op jit(solution)/shard_map/all_to_all | solution.py:261
  56.9 14.2 %collective-permute-start.1 = (bf16[128,128]{1,0:T(8,128)(2,1)S(1)}, bf16[128,128]{1,0:T(8,128)(2,1)S(1)}, u32[]{:S(2)}, u32[]{:S(2)}) collective-permute-start(bf16[128,128]{1,0:T(8,128)(2,1)S(1)} %fusion), channel_id=1, source_target_pairs={{18,0},{82,1},{146,2},{210,3},{274,4},{338,5},{402,6},{466,7},{34,... | collective-permute-start | bytes 98312 | tf_op jit(solution)/shard_map/ppermute | solution.py:269
  67.4 11.0 %all-to-all-start.2 = ((bf16[32,16,128]{2,1,0:T(8,128)(2,1)}), bf16[32,16,128]{2,1,0:T(8,128)(2,1)S(1)}, u32[]{:S(2)}, u32[]{:S(2)}) async-start(bf16[32,16,128]{2,1,0:T(8,128)(2,1)} %get-tuple-element.13), calls=%async_computation.2 | async-start | bytes 262144 | tf_op jit(solution)/shard_map/all_to_all | solution.py:271

commit v7 on v6

--- a/solution.py
+++ b/solution.py
@@ -174,6 +174,46 @@
             image_out[f * groups + k] = image_part[f * size : (f + 1) * size, k * LANES : (k + 1) * LANES]
 
 
+def pack_kernel(spec_emb, grad_spec, image, grad, spec_out, pieces, image_ref, sems):
+    width = spec_emb.shape[1]
+    size = image.shape[0]
+    count = pieces.shape[0]
+    places = (
+        (image, image_ref.at[:size]),
+        (grad, image_ref.at[size:]),
+        (spec_emb, spec_out.at[:, :width]),
+        (grad_spec, spec_out.at[:, width:]),
+    )
+    copies = [pltpu.make_async_copy(a, b, sems.at[n]) for n, (a, b) in enumerate(places)]
+    for copy in copies:
+        copy.start()
+    for copy in copies:
+        copy.wait()
+    for core in range(2):
+        value = image_ref[:, core * LANES : (core + 1) * LANES]
+        for k in range(count):
+            if k // (count // 4) % 2 == core:
+                pieces[k] = value
+
+
+def packed(spec_emb, grad_spec, image, grad, peers):
+    rows, width = spec_emb.shape
+    size, tokens = image.shape
+    return pl.pallas_call(
+        pack_kernel,
+        out_shape=(
+            jax.ShapeDtypeStruct((rows, 2 * width), jnp.bfloat16),
+            jax.ShapeDtypeStruct((peers, 2 * size, LANES), jnp.bfloat16),
+        ),
+        in_specs=(pl.BlockSpec(memory_space=pltpu.HBM),) * 4,
+        compiler_params=pltpu.CompilerParams(vmem_limit_bytes=60 * 2**20),
+        scratch_shapes=[
+            pltpu.VMEM((2 * size, tokens), jnp.bfloat16),
+            pltpu.SemaphoreType.DMA((4,)),
+        ],
+    )(spec_emb, grad_spec, image, grad)
+
+
 def statistics(both, pieces, peers):
     rows, tokens = both.shape[0], pieces.shape[0] // 4 * LANES
     wide = pltpu.VMEM((rows, tokens), jnp.float32)
@@ -245,17 +285,14 @@
     tokens = img_emb.shape[0]
     half = tokens // 2
     second = lax.axis_index("co") == 1
-    own = lax.all_gather(jnp.concatenate([spec_emb, grad_spec], axis=1), "co", tiled=True)
+    own, image = packed(spec_emb, grad_spec, img_emb.T, grad_img.T, 32)
+    image = lax.all_to_all(image, GROUP, 0, 0, tiled=True)
+    own = lax.all_gather(own, "co", tiled=True)
     own = jnp.concatenate(
         [jnp.where(second, a[:, SIZE:], a[:, :SIZE]) for a in (own[:, : 2 * SIZE], own[:, 2 * SIZE :])],
         axis=1,
     )
     own = lax.ppermute(own, EVERY, moves)
-    features = 2 * img_emb.shape[1]
-    image = jnp.concatenate([img_emb, grad_img], axis=1).T.reshape(features, 2, half)
-    image = jnp.moveaxis(image, 1, 0)[None, :, None]
-    image = jnp.broadcast_to(image, (2, 2, 8, features, half)).reshape(32, features, half)
-    image = lax.all_to_all(image, GROUP, 0, 0, tiled=True)
     both = lax.all_gather(own, "co", tiled=True)
     column_part, row_part = statistics(both, image, 16)
     column_parts = lax.all_to_all(column_part, ROWS, 0, 0, tiled=True)

time: 79.7 us -> 79.1 us (level)
  Pallas kernels: 5.93 us -> 7.51 us
  other arithmetic: 2.61 us -> 1.1 us
    pallas_call x0 -> x1, Pallas kernels: none -> 1.57 us  [packed(): pl.pallas_call(pack_kernel, out_shape=(jax.ShapeDtypeStruct((rows, 2 * wi...]
  transfers between devices with their start and end apart: 5 -> 5, of which waited for: 3 -> 3; matrix products, arithmetic and copies ran while one was open for 3% -> 2% of each run, Pallas kernels for 2% -> 2%
where the time goes in v7:
time: 79.1 us; the launch traced here: 78.6 us
  starting transfers between devices  39.5 us (50%)
  waiting for transfers between devices  16.4 us (21%)
  blocking collectives  12.6 us (16%)
  Pallas kernels  7.51 us (9%)
  other arithmetic  1.1 us (1%)
    ppermute x1, starting transfers between devices, shards(): spec_back = lax.ppermute(spec_sum, EVERY, [(b, a) for a, b in moves])  10.5 us
    all_to_all x1, starting transfers between devices, shards(): image = lax.all_to_all(image, GROUP, 0, 0, tiled=True)  10.4 us
    all_to_all x1, starting transfers between devices, shards(): column_parts = lax.all_to_all(column_part, ROWS, 0, 0, tiled=True)  9.08 us
    ppermute x1, waiting for transfers between devices, shards(): own = lax.ppermute(own, EVERY, moves)  8.27 us
    ppermute x1, starting transfers between devices, shards(): own = lax.ppermute(own, EVERY, moves)  5.74 us
    all_to_all x1, waiting for transfers between devices, shards(): image_parts = lax.all_to_all(image_part, GROUP, 0, 0, tiled=True)  4.65 us
    all_to_all x1, starting transfers between devices, shards(): image_parts = lax.all_to_all(image_part, GROUP, 0, 0, tiled=True)  3.69 us
    all_to_all x1, waiting for transfers between devices, shards(): column_parts = lax.all_to_all(column_part, ROWS, 0, 0, tiled=True)  3.46 us
  transfers between devices with their start and end apart: 5, of which 3 were waited for; matrix products, arithmetic and copies ran while one was open for 2% of the time, Pallas kernels for 2%

profile of v7, /device:TPU:1, one launch (start us, length us, event | category | flops | bytes accessed | tf_op | source)
XLA Modules:
  0.0 78.6 jit_solution(2888407158154171987)
XLA Ops:
  0.6 1.6 %shard_map.59 = (bf16[128,256]{1,0:T(8,128)(2,1)}, bf16[32,32,128]{2,1,0:T(8,128)(2,1)}) custom-call(bf16[128,128]{1,0:T(8,128)(2,1)} %spec_emb.1, bf16[128,128]{1,0:T(8,128)(2,1)} %grad_spec.1, bf16[16,256]{1,0:T(8,128)(2,1)} %bitcast.46, bf16[16,256]{1,0:T(8,128)(2,1)} %bitcast.47), custom_call_target="tpu_custom_call" | custom-call | tf_op jit(solution)/shard_map/pallas_call | solution.py:202
  2.2 10.4 %all-to-all-start = ((bf16[32,32,128]{2,1,0:T(8,128)(2,1)}), bf16[32,32,128]{2,1,0:T(8,128)(2,1)S(1)}, u32[]{:S(2)}, u32[]{:S(2)}) async-start(bf16[32,32,128]{2,1,0:T(8,128)(2,1)} %get-tuple-element.11), calls=%async_computation | async-start | bytes 524288 | tf_op jit(solution)/shard_map/all_to_all | solution.py:289
  12.6 2.1 %all_gather.24 = bf16[256,256]{1,0:T(8,128)(2,1)S(1)} all-gather(bf16[128,256]{1,0:T(8,128)(2,1)} %get-tuple-element.10), channel_id=1, replica_groups=mesh['xh'=2,'z3'=2,'z2'=2,'z1'=2,'z0'=2,'co'=2,'xl'=2,'y1'=2,'y0'=2] {'co'}, dimensions={0}, use_global_device_ids=true | all-gather | bytes 196608 | tf_op jit(solution)/shard_map/all_gather | solution.py:290
  14.8 0.1 slice_select_fusion.3
  14.9 0.1 pad_maximum_fusion
  15.0 5.7 %collective-permute-start = (bf16[256,128]{1,0:T(8,128)(2,1)S(1)}, bf16[256,128]{1,0:T(8,128)(2,1)S(1)}, u32[]{:S(2)}, u32[]{:S(2)}) collective-permute-start(bf16[256,128]{1,0:T(8,128)(2,1)S(1)} %pad_maximum_fusion), channel_id=1, source_target_pairs={{0,18},{1,82},{2,146},{3,210},{4,274},{5,338},{6,402},{7,466},{8,3... | collective-permute-start | bytes 196616 | tf_op jit(solution)/shard_map/ppermute | solution.py:295
  20.7 8.3 %collective-permute-done = bf16[256,128]{1,0:T(8,128)(2,1)S(1)} collective-permute-done((bf16[256,128]{1,0:T(8,128)(2,1)S(1)}, bf16[256,128]{1,0:T(8,128)(2,1)S(1)}, u32[]{:S(2)}, u32[]{:S(2)}) %collective-permute-start) | collective-permute-done | bytes 65568 | tf_op jit(solution)/shard_map/ppermute | solution.py:295
  29.0 3.3 %all_gather.25.both = bf16[512,128]{1,0:T(8,128)(2,1)S(1)} all-gather(bf16[256,128]{1,0:T(8,128)(2,1)S(1)} %collective-permute-done), channel_id=1, replica_groups=mesh['xh'=2,'z3'=2,'z2'=2,'z1'=2,'z0'=2,'co'=2,'xl'=2,'y1'=2,'y0'=2] {'co'}, dimensions={0}, use_global_device_ids=true | all-gather | bytes 196608 | tf_op jit(solution)/shard_map/all_gather | solution.py:296
  32.3 0.0 all-to-all-done.pieces
  32.3 2.4 %shard_map.60 = (f32[16,24,128]{2,1,0:T(8,128)}, f32[8,512]{1,0:T(8,128)S(1)}) custom-call(bf16[512,128]{1,0:T(8,128)(2,1)S(1)} %all_gather.25.both, bf16[32,32,128]{2,1,0:T(8,128)(2,1)S(1)} %all-to-all-done.pieces), custom_call_target="tpu_custom_call" | custom-call | tf_op jit(solution)/shard_map/pallas_call | solution.py:221
  34.7 9.1 %all-to-all-start.1 = ((f32[16,24,128]{2,1,0:T(8,128)}), f32[16,24,128]{2,1,0:T(8,128)S(1)}, u32[]{:S(2)}, u32[]{:S(2)}) async-start(f32[16,24,128]{2,1,0:T(8,128)} %get-tuple-element.12), calls=%async_computation.1 | async-start | bytes 393216 | tf_op jit(solution)/shard_map/all_to_all | solution.py:298
  43.8 2.1 %all-gather = f32[16,512]{1,0:T(8,128)S(1)} all-gather(f32[8,512]{1,0:T(8,128)S(1)} %get-tuple-element.13), channel_id=2, replica_groups=mesh['xh'=2,'z3'=2,'z2'=2,'z1'=2,'z0'=2,'co'=2,'xl'=2,'y1'=2,'y0'=2] {'co'}, dimensions={0}, use_global_device_ids=true | all-gather | bytes 49152 | tf_op jit(solution)/shard_map/all_gather | solution.py:299
  46.0 0.1 copy.18.row_ref
  46.1 1.2 %shard_map.61 = (f32[512,1024]{1,0:T(8,128)S(1)}, f32[64,1024]{1,0:T(8,128)S(1)}) custom-call(bf16[512,128]{1,0:T(8,128)(2,1)S(1)} %all_gather.25.both, bf16[32,32,128]{2,1,0:T(8,128)(2,1)S(1)} %all-to-all-done.pieces, f32[512,3]{1,0:T(8,128)S(1)} %copy.18.row_ref), custom_call_target="tpu_custom_call" | custom-call | tf_op jit(solution)/shard_map/pallas_call | solution.py:242
  47.3 3.5 %all-to-all-done.1.column_ref = f32[16,24,128]{2,1,0:T(8,128)S(1)} async-done(((f32[16,24,128]{2,1,0:T(8,128)}), f32[16,24,128]{2,1,0:T(8,128)S(1)}, u32[]{:S(2)}, u32[]{:S(2)}) %all-to-all-start.1) | async-done | bytes 196640 | tf_op jit(solution)/shard_map/all_to_all | solution.py:298
  50.8 2.4 %shard_map.62 = (bf16[2,128,128]{2,1,0:T(8,128)(2,1)S(1)}, bf16[32,16,128]{2,1,0:T(8,128)(2,1)}) custom-call(bf16[512,128]{1,0:T(8,128)(2,1)S(1)} %all_gather.25.both, bf16[32,32,128]{2,1,0:T(8,128)(2,1)S(1)} %all-to-all-done.pieces, f32[16,24,128]{2,1,0:T(8,128)S(1)} %all-to-all-done.1.column_ref, f32[512,1024]{1,0:T(8,128)S(1)} %get-tuple-element.14.row_slope, ...), custom_call_target="tpu_custom_call" | custom-call | tf_op jit(solution)/shard_map/pallas_call | solution.py:261
  53.2 3.2 %all-gather.1 = bf16[4,128,128]{2,1,0:T(8,128)(2,1)S(1)} all-gather(bf16[2,128,128]{2,1,0:T(8,128)(2,1)S(1)} %get-tuple-element.16), channel_id=3, replica_groups=mesh['xh'=2,'z3'=2,'z2'=2,'z1'=2,'z0'=2,'co'=2,'xl'=2,'y1'=2,'y0'=2] {'co'}, dimensions={0}, use_global_device_ids=true | all-gather | bytes 196608 | tf_op jit(solution)/shard_map/all_gather | solution.py:303
  56.4 10.5 %collective-permute-start.1 = (bf16[128,128]{1,0:T(8,128)(2,1)S(1)}, bf16[128,128]{1,0:T(8,128)(2,1)S(1)}, u32[]{:S(2)}, u32[]{:S(2)}) collective-permute-start(bf16[128,128]{1,0:T(8,128)(2,1)S(1)} %fusion), channel_id=1, source_target_pairs={{18,0},{82,1},{146,2},{210,3},{274,4},{338,5},{402,6},{466,7},{34,... | collective-permute-start | bytes 98312 | tf_op jit(solution)/shard_map/ppermute | solution.py:306
  66.9 3.7 %all-to-all-start.2 = ((bf16[32,16,128]{2,1,0:T(8,128)(2,1)}), bf16[32,16,128]{2,1,0:T(8,128)(2,1)S(1)}, u32[]{:S(2)}, u32[]{:S(2)}) async-start(bf16[32,16,128]{2,1,0:T(8,128)(2,1)} %get-tuple-element.17), calls=%async_computation.2 | async-start | bytes 262144 | tf_op jit(solution)/shard_map/all_to_all | solution.py:308
  70.6 0.0 collective-permute-done.1
  70.7 1.9 %all-gather.2 = bf16[256,128]{1,0:T(8,128)(2,1)S(1)} all-gather(bf16[128,128]{1,0:T(8,128)(2,1)S(1)} %collective-permute-done.1), channel_id=4, replica_groups=mesh['xh'=2,'z3'=2,'z2'=2,'z1'=2,'z0'=2,'co'=2,'xl'=2,'y1'=2,'y0'=2] {'co'}, dimensions={0}, use_global_device_ids=true | all-gather | bytes 98304 | tf_op jit(solution)/shard_map/all_gather | solution.py:313
  72.5 0.1 slice_select_fusion
  72.6 0.7 pad_maximum_fusion.1
  73.3 4.7 %all-to-all-done.2 = bf16[32,16,128]{2,1,0:T(8,128)(2,1)S(1)} async-done(((bf16[32,16,128]{2,1,0:T(8,128)(2,1)}), bf16[32,16,128]{2,1,0:T(8,128)(2,1)S(1)}, u32[]{:S(2)}, u32[]{:S(2)}) %all-to-all-start.2) | async-done | bytes 131104 | tf_op jit(solution)/shard_map/all_to_all | solution.py:308
  78.0 0.6 copy_bitcast_fusion
  (8 shorter events, 0.1 us)
Async XLA Ops:
  2.2 30.1 %all-to-all-start = ((bf16[32,32,128]{2,1,0:T(8,128)(2,1)}), bf16[32,32,128]{2,1,0:T(8,128)(2,1)S(1)}, u32[]{:S(2)}, u32[]{:S(2)}) async-start(bf16[32,32,128]{2,1,0:T(8,128)(2,1)} %get-tuple-element.11), calls=%async_computation | async-start | bytes 524288 | tf_op jit(solution)/shard_map/all_to_all | solution.py:289
  15.0 14.0 %collective-permute-start = (bf16[256,128]{1,0:T(8,128)(2,1)S(1)}, bf16[256,128]{1,0:T(8,128)(2,1)S(1)}, u32[]{:S(2)}, u32[]{:S(2)}) collective-permute-start(bf16[256,128]{1,0:T(8,128)(2,1)S(1)} %pad_maximum_fusion), channel_id=1, source_target_pairs={{0,18},{1,82},{2,146},{3,210},{4,274},{5,338},{6,402},{7,466},{8,3... | collective-permute-start | bytes 196616 | tf_op jit(solution)/shard_map/ppermute | solution.py:295
  34.7 16.1 %all-to-all-start.1 = ((f32[16,24,128]{2,1,0:T(8,128)}), f32[16,24,128]{2,1,0:T(8,128)S(1)}, u32[]{:S(2)}, u32[]{:S(2)}) async-start(f32[16,24,128]{2,1,0:T(8,128)} %get-tuple-element.12), calls=%async_computation.1 | async-start | bytes 393216 | tf_op jit(solution)/shard_map/all_to_all | solution.py:298
  56.4 14.2 %collective-permute-start.1 = (bf16[128,128]{1,0:T(8,128)(2,1)S(1)}, bf16[128,128]{1,0:T(8,128)(2,1)S(1)}, u32[]{:S(2)}, u32[]{:S(2)}) collective-permute-start(bf16[128,128]{1,0:T(8,128)(2,1)S(1)} %fusion), channel_id=1, source_target_pairs={{18,0},{82,1},{146,2},{210,3},{274,4},{338,5},{402,6},{466,7},{34,... | collective-permute-start | bytes 98312 | tf_op jit(solution)/shard_map/ppermute | solution.py:306
  66.9 11.0 %all-to-all-start.2 = ((bf16[32,16,128]{2,1,0:T(8,128)(2,1)}), bf16[32,16,128]{2,1,0:T(8,128)(2,1)S(1)}, u32[]{:S(2)}, u32[]{:S(2)}) async-start(bf16[32,16,128]{2,1,0:T(8,128)(2,1)} %get-tuple-element.17), calls=%async_computation.2 | async-start | bytes 262144 | tf_op jit(solution)/shard_map/all_to_all | solution.py:308
